TPU v7x, 128 devices: a whole 4x4x4 slice. The times are simulated.
128 devices in a mesh: tile: 32 (over z, y, core), sub: 4 (over x).
Axes of the slice: x: 4, y: 4, z: 4, core: 2. Of those that a mesh axis runs over, the one named last changes fastest.
Arguments:
- offsets: float32 [3, 32, 64, 1024], P(None, None, 'tile', 'sub'), may hold values from 0 to 1
- velocity: float32 [3, 32, 64, 1024], P(None, None, 'tile', 'sub'), may hold values from -1.5 to 1.5
- mass: float32 [32, 64, 1024], P(None, 'tile', 'sub'), may hold values from 0.015625 to 0.0625
- entropy: float32 [32, 64, 1024], P(None, 'tile', 'sub'), may hold values from 0.5 to 2
- active_counts: int32 [3, 64, 1024], P(None, 'tile', 'sub'), may hold values from 0 to 32, as said below
- targets: int32 [32, 64, 1024], P(None, 'tile', 'sub'), may hold values from 0 to 3, as said below
Outputs:
- arrived: float32 [8, 3145728], P(None, ('tile', 'sub'))
Inputs may be any that keep to these rules, and one draw needn't show every extreme that they name: active_counts[0] is a cell's number of occupied slots, from 16 to 32; counts never rise from one level to the next; active_counts[1] is at most 16 and active_counts[2] at most 8, and these bounds and 32 are each reached in some cell. Active particles of a substep are the cell's first slots. `targets`: among one device's 16384 particles, no destination is named by more than 6144 of them, and one destination is named by exactly 6144.
All inputs are finite; a program needn't handle non-finite values.
Results may differ from a plain program's by a relative error of at most 0.0001.
Values sent between devices are 32-bit elements; how exact they have to be, the bound alone decides.
A program may use at most 128 MiB of HBM per device.

v0:
```python
import math

import jax
import jax.numpy as jnp
from jax import lax
from jax.sharding import PartitionSpec as P

LEVELS = 3


KERNEL_NORM = 21.0 / (2.0 * math.pi)
GAMMA = 5.0 / 3.0
VISC_ALPHA = 1.0
VISC_BETA = 2.0
TIME_STEP = 0.05
SOFTEN = 0.01


def with_halo(cells, sides, width):
    for axis, dim in sides:
        count = lax.axis_size(axis)
        head = lax.slice_in_dim(cells, 0, width, axis=dim)
        tail = lax.slice_in_dim(cells, cells.shape[dim] - width, cells.shape[dim], axis=dim)
        cells = jnp.concatenate(
            [
                lax.ppermute(tail, axis, [(i, (i + 1) % count) for i in range(count)]),
                cells,
                lax.ppermute(head, axis, [((i + 1) % count, i) for i in range(count)]),
            ],
            axis=dim,
        )
    return cells


def separation(local_part, theirs, shift_x, shift_y):
    delta_x = local_part[0][:, None] - theirs[0][None, :] - shift_x
    delta_y = local_part[1][:, None] - theirs[1][None, :] - shift_y
    delta_z = local_part[2][:, None] - theirs[2][None, :]
    return (delta_x, delta_y, delta_z)


def density_pair(local_part, theirs, shift_x, shift_y):
    delta_x, delta_y, delta_z = separation(local_part, theirs, shift_x, shift_y)
    squared = delta_x * delta_x + delta_y * delta_y + delta_z * delta_z
    radius = jnp.sqrt(squared)
    remain = jnp.maximum(1.0 - radius, 0.0)
    weight = KERNEL_NORM * remain**4 * (1.0 + 4.0 * radius)
    return jnp.sum(theirs[6][None, :] * weight, axis=1)


def force_pair(local_part, theirs, own_pressure, their_pressure, shift_x, shift_y):
    delta_x, delta_y, delta_z = separation(local_part, theirs, shift_x, shift_y)
    squared = delta_x * delta_x + delta_y * delta_y + delta_z * delta_z
    radius = jnp.sqrt(squared)
    remain = jnp.maximum(1.0 - radius, 0.0)
    relative_x = local_part[3][:, None] - theirs[3][None, :]
    relative_y = local_part[4][:, None] - theirs[4][None, :]
    relative_z = local_part[5][:, None] - theirs[5][None, :]
    approach = delta_x * relative_x + delta_y * relative_y + delta_z * relative_z
    closing = jnp.minimum(approach, 0.0) / (squared + SOFTEN)
    sound_mean = 0.5 * (own_pressure[1][:, None] + their_pressure[1][None, :])
    mean_density = 0.5 * (own_pressure[2][:, None] + their_pressure[2][None, :])
    viscous = (-VISC_ALPHA * sound_mean * closing + VISC_BETA * closing * closing) / mean_density
    strength = theirs[6][None, :] * (
        own_pressure[0][:, None] + their_pressure[0][None, :] + viscous
    )
    strength = strength * (20.0 * KERNEL_NORM) * remain**3
    return jnp.stack(
        [
            jnp.sum(strength * delta_x, axis=1),
            jnp.sum(strength * delta_y, axis=1),
            jnp.sum(strength * delta_z, axis=1),
        ]
    )


def pressure_terms(density, entropy, occupied):
    density_used = jnp.where(occupied, density, 1.0)
    return jnp.stack(
        [
            entropy * density_used ** (GAMMA - 2.0),
            jnp.sqrt(GAMMA * entropy * density_used ** (GAMMA - 1.0)),
            density_used,
        ]
    )


def neighbour_view(ghosts, shift_x, shift_y, width_x, width_y):
    return ghosts[:, :, 1 + shift_x : 1 + shift_x + width_x, 1 + shift_y : 1 + shift_y + width_y]


def local_density(motion, ghosts):
    width_x, width_y = (motion.shape[2], motion.shape[3])
    summed = jnp.zeros(motion.shape[1:], jnp.float32)
    for shift_x in (-1, 0, 1):
        for shift_y in (-1, 0, 1):
            theirs = neighbour_view(ghosts, shift_x, shift_y, width_x, width_y)
            summed = summed + density_pair(motion, theirs, float(shift_x), float(shift_y))
    return summed


def local_force(motion, ghosts, pressure, pressure_ghosts):
    width_x, width_y = (motion.shape[2], motion.shape[3])
    summed = jnp.zeros((3,) + motion.shape[1:], jnp.float32)
    for shift_x in (-1, 0, 1):
        for shift_y in (-1, 0, 1):
            theirs = neighbour_view(ghosts, shift_x, shift_y, width_x, width_y)
            their_pressure = neighbour_view(pressure_ghosts, shift_x, shift_y, width_x, width_y)
            summed = summed + force_pair(
                motion, theirs, pressure, their_pressure, float(shift_x), float(shift_y)
            )
    return summed


def share_motion(motion):
    return with_halo(motion, (("tile", 2), ("sub", 3)), 1)


def share_pressure(pressure):
    received = with_halo(pressure, (("tile", 2), ("sub", 3)), 1)
    return (received, received)


def shards(offsets, velocity, mass, entropy, active_counts, targets):
    slots, width_x, width_y = mass.shape
    slot_index = lax.broadcasted_iota(jnp.int32, (slots, width_x, width_y), 0)
    occupied = slot_index < active_counts[0][None]
    mass_live = jnp.where(occupied, mass, 0.0)
    places = offsets
    speeds = velocity
    density = jnp.ones((slots, width_x, width_y), jnp.float32)
    motion_ghosts = None
    for substep in range(LEVELS):
        active = slot_index < active_counts[substep][None]
        motion = jnp.concatenate([places, speeds, mass_live[None]], axis=0)
        motion_ghosts = share_motion(motion)
        fresh_density = local_density(motion, motion_ghosts)
        density = jnp.where(active, fresh_density, density)
        pressure = pressure_terms(density, entropy, occupied)
        pressure_ghosts, carried = share_pressure(pressure)
        acceleration = local_force(motion, motion_ghosts, pressure, pressure_ghosts)
        speeds = jnp.where(active[None], speeds + TIME_STEP * acceleration, speeds)
        places = jnp.where(active[None], places + TIME_STEP * speeds, places)
    particle_state = jnp.concatenate(
        [places, speeds, density[None], mass_live[None]], axis=0
    ).reshape(8, -1)
    per_device = slots * width_x * width_y
    capacity = 3 * per_device // 8
    sub_count = lax.axis_size("sub")
    destination = targets.reshape(-1)
    onehot = (destination[None, :] == jnp.arange(sub_count, dtype=jnp.int32)[:, None]).astype(
        jnp.int32
    )
    rank_in = jnp.sum((jnp.cumsum(onehot, axis=1) - 1) * onehot, axis=0)
    flat_slot = destination * capacity + rank_in
    buffer = jnp.zeros((8, sub_count * capacity), jnp.float32).at[:, flat_slot].set(particle_state)
    buffer = buffer.reshape(8, sub_count, capacity)
    arrived = lax.all_to_all(buffer, "sub", split_axis=1, concat_axis=1, tiled=True)
    return arrived.reshape(8, sub_count * capacity)


def solution(mesh):
    placed = (
        P(None, None, "tile", "sub"),
        P(None, None, "tile", "sub"),
        P(None, "tile", "sub"),
        P(None, "tile", "sub"),
        P(None, "tile", "sub"),
        P(None, "tile", "sub"),
    )
    return jax.shard_map(
        shards, mesh=mesh, in_specs=placed, out_specs=P(None, ("tile", "sub")), check_vma=False
    )
```

profile of v0, /device:TPU:0, one launch (start us, length us, event | category | flops | bytes accessed | tf_op | source)
XLA Modules:
  0.0 413.2 jit_solution(13906708602313657745)
XLA Ops:
  3.4 6.1 %collective-permute-start.1 = (f32[7,32,1,256]{3,2,1,0:T(1,128)S(1)}, f32[7,32,1,256]{3,2,1,0:T(1,128)S(1)}, u32[]{:S(2)}, u32[]{:S(2)}) collective-permute-start(f32[7,32,1,256]{3,2,1,0:T(1,128)S(1)} %get-tuple-element.425), channel_id=1, source_target_pairs={{4,0},{8,4},{12,8},{16,12},{20,16},{24,20},{28,24},{32,28},{36,32}... | collective-permute-start | bytes 688136 | tf_op jit(solution)/shard_map/ppermute | solution.py:28
  19.4 6.2 %collective-permute-done.2 = f32[7,32,4,1]{3,2,1,0:T(4,128)S(1)} collective-permute-done((f32[7,32,4,1]{3,2,1,0:T(4,128)S(1)}, f32[7,32,4,1]{3,2,1,0:T(4,128)S(1)}, u32[]{:S(2)}, u32[]{:S(2)}) %collective-permute-start.2) | collective-permute-done | bytes 3616 | tf_op jit(solution)/shard_map/ppermute | solution.py:26
  35.7 7.7 %fusion.10 = (f32[32,2,256]{2,1,0:T(2,128)S(1)}, f32[32,2,256]{2,1,0:T(2,128)S(1)}, f32[32,2,256]{2,1,0:T(2,128)S(1)}, f32[32,2,256]{2,1,0:T(2,128)S(1)}) fusion(f32[32,2,256]{2,0,1:T(8,128)S(1)} %copy.29, f32[32,2,256]{2,0,1:T(8,128)S(1)} %copy.28, f32[32,2,256]{2,0,1:T(8,128)S(1)} %copy.27, f32[32,2,256]{2,0,1:T(8,128)S(1)} %copy.26, ...), kind=kLoop, calls=%fused_computation.206 | loop fusion | flops 39780352 | bytes 1507328 | tf_op jit(solution)/shard_map/reduce_sum | solution.py:48
  43.5 7.8 %fusion.5 = (f32[32,2,256]{2,1,0:T(2,128)S(1)}, f32[32,2,256]{2,1,0:T(2,128)S(1)}, f32[32,2,256]{2,1,0:T(2,128)S(1)}, f32[32,2,256]{2,1,0:T(2,128)S(1)}) fusion(f32[32,2,256]{2,0,1:T(8,128)S(1)} %copy.25, f32[32,2,256]{2,1,0:T(2,128)S(1)} %get-tuple-element.478, f32[32,2,256]{2,0,1:T(8,128)S(1)} %copy.24, f32[32,2,256]{2,1,0:T(2,128)S(1)} %get-tuple-element.479, ...), kind=kLoop, calls=%fused_computation.201 | loop fusion | flops 40828928 | bytes 1507328 | tf_op jit(solution)/shard_map/reduce_sum | solution.py:48
  53.4 5.3 %collective-permute-start.5 = (f32[3,32,1,256]{3,2,1,0:T(1,128)}, f32[3,32,1,256]{3,2,1,0:T(1,128)S(1)}, u32[]{:S(2)}, u32[]{:S(2)}) collective-permute-start(f32[3,32,1,256]{3,2,1,0:T(1,128)} %get-tuple-element.476), channel_id=1, source_target_pairs={{4,0},{8,4},{12,8},{16,12},{20,16},{24,20},{28,24},{32,28},{36,32}... | collective-permute-start | bytes 294920 | tf_op jit(solution)/shard_map/ppermute | solution.py:28
  81.1 17.5 %multiply_reduce_fusion.25 = (f32[32,2,256]{2,1,0:T(2,128)S(1)}, f32[32,2,256]{2,1,0:T(2,128)S(1)}, f32[32,2,256]{2,1,0:T(2,128)S(1)}, f32[32,2,256]{2,1,0:T(2,1...) fusion(f32[32,2,256]{2,0,1:T(8,128)S(1)} %copy-done.28, ...), kind=kLoop, calls=%fused_computation.697 | loop fusion | flops 89980928 | bytes 3997696 | tf_op jit(solution)/shard_map/reduce_sum | solution.py:70
  98.6 17.2 %multiply_reduce_fusion.26 = (f32[32,2,256]{2,1,0:T(2,128)S(1)}, f32[32,2,256]{2,1,0:T(2,128)S(1)}, f32[32,2,256]{2,1,0:T(2,128)S(1)}, f32[32,2,256]{2,1,0:T(2,1...) fusion(f32[32,2,256]{2,0,1:T(8,128)S(1)} %copy.51, ...), kind=kLoop, calls=%fused_computation.698 | loop fusion | flops 91029504 | bytes 3997696 | tf_op jit(solution)/shard_map/reduce_sum | solution.py:70
  117.5 5.1 %collective-permute-start.9 = (f32[7,32,1,256]{3,2,1,0:T(1,128)S(1)}, f32[7,32,1,256]{3,2,1,0:T(1,128)S(1)}, u32[]{:S(2)}, u32[]{:S(2)}) collective-permute-start(f32[7,32,1,256]{3,2,1,0:T(1,128)S(1)} %get-tuple-element.421), channel_id=1, source_target_pairs={{4,0},{8,4},{12,8},{16,12},{20,16},{24,20},{28,24},{32,28},{36,32}... | collective-permute-start | bytes 688136 | tf_op jit(solution)/shard_map/ppermute | solution.py:28
  131.7 5.2 %collective-permute-done.10 = f32[7,32,4,1]{3,2,1,0:T(4,128)S(1)} collective-permute-done((f32[7,32,4,1]{3,2,1,0:T(4,128)S(1)}, f32[7,32,4,1]{3,2,1,0:T(4,128)S(1)}, u32[]{:S(2)}, u32[]{:S(2)}) %collective-permute-start.10) | collective-permute-done | bytes 3616 | tf_op jit(solution)/shard_map/ppermute | solution.py:26
  144.9 7.7 %fusion.55 = (f32[32,2,256]{2,1,0:T(2,128)S(1)}, f32[32,2,256]{2,1,0:T(2,128)S(1)}, f32[32,2,256]{2,1,0:T(2,128)S(1)}, f32[32,2,256]{2,1,0:T(2,128)S(1)}) fusion(f32[32,2,256]{2,0,1:T(8,128)S(1)} %copy.119, f32[32,2,256]{2,0,1:T(8,128)S(1)} %copy.118, f32[32,2,256]{2,0,1:T(8,128)S(1)} %copy.117, f32[32,2,256]{2,0,1:T(8,128)S(1)} %copy.116, ...), kind=kLoop, calls=%fused_computation.251 | loop fusion | flops 39780352 | bytes 1507328 | tf_op jit(solution)/shard_map/reduce_sum | solution.py:48
  152.6 7.9 %fusion.50 = (f32[32,2,256]{2,1,0:T(2,128)S(1)}, f32[32,2,256]{2,1,0:T(2,128)S(1)}, f32[32,2,256]{2,1,0:T(2,128)S(1)}, f32[32,2,256]{2,1,0:T(2,128)S(1)}) fusion(f32[32,2,256]{2,0,1:T(8,128)S(1)} %copy.115, f32[32,2,256]{2,1,0:T(2,128)S(1)} %get-tuple-element.470, f32[32,2,256]{2,0,1:T(8,128)S(1)} %copy.114, f32[32,2,256]{2,1,0:T(2,128)S(1)} %get-tuple-element.471, ...), kind=kLoop, calls=%fused_computation.246 | loop fusion | flops 40828928 | bytes 1507328 | tf_op jit(solution)/shard_map/reduce_sum | solution.py:48
  161.8 5.1 %collective-permute-start.13 = (f32[3,32,1,256]{3,2,1,0:T(1,128)S(1)}, f32[3,32,1,256]{3,2,1,0:T(1,128)S(1)}, u32[]{:S(2)}, u32[]{:S(2)}) collective-permute-start(f32[3,32,1,256]{3,2,1,0:T(1,128)S(1)} %get-tuple-element.468), channel_id=1, source_target_pairs={{4,0},{8,4},{12,8},{16,12},{20,16},{24,20},{28,24},{32,28},{36,32}... | collective-permute-start | bytes 294920 | tf_op jit(solution)/shard_map/ppermute | solution.py:28
  184.1 17.6 %multiply_reduce_fusion.13 = (f32[32,2,256]{2,1,0:T(2,128)S(1)}, f32[32,2,256]{2,1,0:T(2,128)S(1)}, f32[32,2,256]{2,1,0:T(2,128)S(1)}, f32[32,2,256]{2,1,0:T(2,1...) fusion(f32[32,2,256]{2,0,1:T(8,128)S(1)} %copy.144, ...), kind=kLoop, calls=%fused_computation.664 | loop fusion | flops 89980928 | bytes 3997696 | tf_op jit(solution)/shard_map/reduce_sum | solution.py:70
  201.8 17.4 %multiply_reduce_fusion.14 = (f32[32,2,256]{2,1,0:T(2,128)S(1)}, f32[32,2,256]{2,1,0:T(2,128)S(1)}, f32[32,2,256]{2,1,0:T(2,128)S(1)}, f32[32,2,256]{2,1,0:T(2,1...) fusion(f32[32,2,256]{2,0,1:T(8,128)S(1)} %copy.140, ...), kind=kLoop, calls=%fused_computation.665 | loop fusion | flops 91029504 | bytes 3997696 | tf_op jit(solution)/shard_map/reduce_sum | solution.py:70
  235.1 5.2 %collective-permute-done.18 = f32[7,32,4,1]{3,2,1,0:T(4,128)S(1)} collective-permute-done((f32[7,32,4,1]{3,2,1,0:T(4,128)S(1)}, f32[7,32,4,1]{3,2,1,0:T(4,128)S(1)}, u32[]{:S(2)}, u32[]{:S(2)}) %collective-permute-start.18) | collective-permute-done | bytes 3616 | tf_op jit(solution)/shard_map/ppermute | solution.py:26
  248.5 7.7 %fusion.100 = (f32[32,2,256]{2,1,0:T(2,128)S(1)}, f32[32,2,256]{2,1,0:T(2,128)S(1)}, f32[32,2,256]{2,1,0:T(2,128)S(1)}, f32[32,2,256]{2,1,0:T(2,128)S(1)}) fusion(f32[32,2,256]{2,0,1:T(8,128)S(1)} %copy.208, f32[32,2,256]{2,0,1:T(8,128)S(1)} %copy.207, f32[32,2,256]{2,0,1:T(8,128)S(1)} %copy.206, f32[32,2,256]{2,0,1:T(8,128)S(1)} %copy.205, ...), kind=kLoop, calls=%fused_computation.296 | loop fusion | flops 39780352 | bytes 1507328 | tf_op jit(solution)/shard_map/reduce_sum | solution.py:48
  256.3 7.8 %fusion.95 = (f32[32,2,256]{2,1,0:T(2,128)S(1)}, f32[32,2,256]{2,1,0:T(2,128)S(1)}, f32[32,2,256]{2,1,0:T(2,128)S(1)}, f32[32,2,256]{2,1,0:T(2,128)S(1)}) fusion(f32[32,2,256]{2,0,1:T(8,128)S(1)} %copy.204, f32[32,2,256]{2,1,0:T(2,128)S(1)} %get-tuple-element.462, f32[32,2,256]{2,0,1:T(8,128)S(1)} %copy.203, f32[32,2,256]{2,1,0:T(2,128)S(1)} %get-tuple-element.463, ...), kind=kLoop, calls=%fused_computation.291 | loop fusion | flops 40828928 | bytes 1507328 | tf_op jit(solution)/shard_map/reduce_sum | solution.py:48
  266.1 5.1 %collective-permute-start.21 = (f32[3,32,1,256]{3,2,1,0:T(1,128)}, f32[3,32,1,256]{3,2,1,0:T(1,128)S(1)}, u32[]{:S(2)}, u32[]{:S(2)}) collective-permute-start(f32[3,32,1,256]{3,2,1,0:T(1,128)} %get-tuple-element.460), channel_id=1, source_target_pairs={{4,0},{8,4},{12,8},{16,12},{20,16},{24,20},{28,24},{32,28},{36,32}... | collective-permute-start | bytes 294920 | tf_op jit(solution)/shard_map/ppermute | solution.py:28
  303.5 17.5 %multiply_reduce_fusion.1 = (f32[32,2,256]{2,1,0:T(2,128)S(1)}, f32[32,2,256]{2,1,0:T(2,128)S(1)}, f32[32,2,256]{2,1,0:T(2,128)S(1)}, f32[32,2,256]{2,1,0:T(2,12...) fusion(f32[32,2,256]{2,0,1:T(8,128)S(1)} %copy-done.8, ...), kind=kLoop, calls=%fused_computation.631 | loop fusion | flops 89980928 | bytes 3997696 | tf_op jit(solution)/shard_map/reduce_sum | solution.py:70
  321.1 17.2 %multiply_reduce_fusion.2 = (f32[32,2,256]{2,1,0:T(2,128)S(1)}, f32[32,2,256]{2,1,0:T(2,128)S(1)}, f32[32,2,256]{2,1,0:T(2,128)S(1)}, f32[32,2,256]{2,1,0:T(2,12...) fusion(f32[32,2,256]{2,0,1:T(8,128)S(1)} %copy.229, ...), kind=kLoop, calls=%fused_computation.632 | loop fusion | flops 91029504 | bytes 3997696 | tf_op jit(solution)/shard_map/reduce_sum | solution.py:70
  340.0 5.2 %copy.290 = f32[16384,8]{1,0:T(8,128)} copy(f32[16384,8]{0,1:T(8,128)S(1)} %maximum_bitcast_fusion) | data formatting | bytes 1048576 | tf_op jit(solution)/shard_map/concatenate | solution.py:144
  345.2 46.0 %scatter_custom_fusion = f32[8,24576]{0,1:T(8,128)} fusion(s32[16384]{0:T(1024)} %bitcast.739, f32[16384,8]{1,0:T(8,128)} %copy.290, f32[]{:T(128)} %constant.90.clone.1), kind=kCustom, calls=%fused_computation.1 | custom fusion | bytes 786944 | tf_op jit(solution)/shard_map/scatter | solution.py:156
  391.2 7.4 %copy.291 = f32[8,4,6144]{2,0,1:T(8,128)S(1)} copy(f32[8,4,6144]{0,2,1:T(8,128)} %bitcast.640) | data formatting | bytes 1572864 | tf_op jit(solution)/shard_map/reshape | solution.py:157
  398.6 13.5 %all_to_all.5 = f32[8,4,6144]{2,0,1:T(8,128)S(1)} all-to-all(f32[8,4,6144]{2,0,1:T(8,128)S(1)} %copy.291), channel_id=1, replica_groups=mesh['tile'=32,'sub'=4] {'sub'}, dimensions={1} | all-to-all | bytes 1572864 | tf_op jit(solution)/shard_map/all_to_all | solution.py:158
  (592 shorter events, 142.9 us)
Async XLA Ops:
  3.3 9.8 %collective-permute-start = (f32[7,32,1,256]{3,2,1,0:T(1,128)S(1)}, f32[7,32,1,256]{3,2,1,0:T(1,128)S(1)}, u32[]{:S(2)}, u32[]{:S(2)}) collective-permute-start(f32[7,32,1,256]{3,2,1,0:T(1,128)S(1)} %get-tuple-element.424), channel_id=1, source_target_pairs={{0,4},{4,8},{8,12},{12,16},{16,20},{20,24},{24,28},{28,32},{32,36}... | collective-permute-start | bytes 688136 | tf_op jit(solution)/shard_map/ppermute | solution.py:26
  3.4 9.7 %collective-permute-start.1 = (f32[7,32,1,256]{3,2,1,0:T(1,128)S(1)}, f32[7,32,1,256]{3,2,1,0:T(1,128)S(1)}, u32[]{:S(2)}, u32[]{:S(2)}) collective-permute-start(f32[7,32,1,256]{3,2,1,0:T(1,128)S(1)} %get-tuple-element.425), channel_id=1, source_target_pairs={{4,0},{8,4},{12,8},{16,12},{20,16},{24,20},{28,24},{32,28},{36,32}... | collective-permute-start | bytes 688136 | tf_op jit(solution)/shard_map/ppermute | solution.py:28
  14.1 11.5 %collective-permute-start.2 = (f32[7,32,4,1]{3,2,1,0:T(4,128)S(1)}, f32[7,32,4,1]{3,2,1,0:T(4,128)S(1)}, u32[]{:S(2)}, u32[]{:S(2)}) collective-permute-start(f32[7,32,4,1]{3,2,1,0:T(4,128)S(1)} %get-tuple-element.358), channel_id=1, source_target_pairs={{0,1},{1,2},{2,3},{3,0},{4,5},{5,6},{6,7},{7,4},{8,9},{9,10},{10,1... | collective-permute-start | bytes 10760 | tf_op jit(solution)/shard_map/ppermute | solution.py:26
  15.6 9.9 %collective-permute-start.3 = (f32[7,32,4,1]{3,2,1,0:T(4,128)S(1)}, f32[7,32,4,1]{3,2,1,0:T(4,128)S(1)}, u32[]{:S(2)}, u32[]{:S(2)}) collective-permute-start(f32[7,32,4,1]{3,2,1,0:T(4,128)S(1)} %get-tuple-element.359), channel_id=1, source_target_pairs={{1,0},{2,1},{3,2},{0,3},{5,4},{6,5},{7,6},{4,7},{9,8},{10,9},{11,1... | collective-permute-start | bytes 10760 | tf_op jit(solution)/shard_map/ppermute | solution.py:28
  53.2 12.9 %collective-permute-start.4 = (f32[3,32,1,256]{3,2,1,0:T(1,128)}, f32[3,32,1,256]{3,2,1,0:T(1,128)S(1)}, u32[]{:S(2)}, u32[]{:S(2)}) collective-permute-start(f32[3,32,1,256]{3,2,1,0:T(1,128)} %get-tuple-element.475), channel_id=1, source_target_pairs={{0,4},{4,8},{8,12},{12,16},{16,20},{20,24},{24,28},{28,32},{32,36}... | collective-permute-start | bytes 294920 | tf_op jit(solution)/shard_map/ppermute | solution.py:26
  53.4 12.7 %collective-permute-start.5 = (f32[3,32,1,256]{3,2,1,0:T(1,128)}, f32[3,32,1,256]{3,2,1,0:T(1,128)S(1)}, u32[]{:S(2)}, u32[]{:S(2)}) collective-permute-start(f32[3,32,1,256]{3,2,1,0:T(1,128)} %get-tuple-element.476), channel_id=1, source_target_pairs={{4,0},{8,4},{12,8},{16,12},{20,16},{24,20},{28,24},{32,28},{36,32}... | collective-permute-start | bytes 294920 | tf_op jit(solution)/shard_map/ppermute | solution.py:28
  66.6 6.9 %collective-permute-start.6 = (f32[3,32,4,1]{3,2,1,0:T(4,128)S(1)}, f32[3,32,4,1]{3,2,1,0:T(4,128)S(1)}, u32[]{:S(2)}, u32[]{:S(2)}) collective-permute-start(f32[3,32,4,1]{3,2,1,0:T(4,128)S(1)} %get-tuple-element.436), channel_id=1, source_target_pairs={{0,1},{1,2},{2,3},{3,0},{4,5},{5,6},{6,7},{7,4},{8,9},{9,10},{10,1... | collective-permute-start | bytes 4616 | tf_op jit(solution)/shard_map/ppermute | solution.py:26
  68.1 5.7 %collective-permute-start.7 = (f32[3,32,4,1]{3,2,1,0:T(4,128)S(1)}, f32[3,32,4,1]{3,2,1,0:T(4,128)S(1)}, u32[]{:S(2)}, u32[]{:S(2)}) collective-permute-start(f32[3,32,4,1]{3,2,1,0:T(4,128)S(1)} %get-tuple-element.437), channel_id=1, source_target_pairs={{1,0},{2,1},{3,2},{0,3},{5,4},{6,5},{7,6},{4,7},{9,8},{10,9},{11,1... | collective-permute-start | bytes 4616 | tf_op jit(solution)/shard_map/ppermute | solution.py:28
  117.4 8.8 %collective-permute-start.8 = (f32[7,32,1,256]{3,2,1,0:T(1,128)S(1)}, f32[7,32,1,256]{3,2,1,0:T(1,128)S(1)}, u32[]{:S(2)}, u32[]{:S(2)}) collective-permute-start(f32[7,32,1,256]{3,2,1,0:T(1,128)S(1)} %get-tuple-element.420), channel_id=1, source_target_pairs={{0,4},{4,8},{8,12},{12,16},{16,20},{20,24},{24,28},{28,32},{32,36}... | collective-permute-start | bytes 688136 | tf_op jit(solution)/shard_map/ppermute | solution.py:26
  117.5 8.8 %collective-permute-start.9 = (f32[7,32,1,256]{3,2,1,0:T(1,128)S(1)}, f32[7,32,1,256]{3,2,1,0:T(1,128)S(1)}, u32[]{:S(2)}, u32[]{:S(2)}) collective-permute-start(f32[7,32,1,256]{3,2,1,0:T(1,128)S(1)} %get-tuple-element.421), channel_id=1, source_target_pairs={{4,0},{8,4},{12,8},{16,12},{20,16},{24,20},{28,24},{32,28},{36,32}... | collective-permute-start | bytes 688136 | tf_op jit(solution)/shard_map/ppermute | solution.py:28
  127.2 9.8 %collective-permute-start.10 = (f32[7,32,4,1]{3,2,1,0:T(4,128)S(1)}, f32[7,32,4,1]{3,2,1,0:T(4,128)S(1)}, u32[]{:S(2)}, u32[]{:S(2)}) collective-permute-start(f32[7,32,4,1]{3,2,1,0:T(4,128)S(1)} %get-tuple-element.340), channel_id=1, source_target_pairs={{0,1},{1,2},{2,3},{3,0},{4,5},{5,6},{6,7},{7,4},{8,9},{9,10},{10,1... | collective-permute-start | bytes 10760 | tf_op jit(solution)/shard_map/ppermute | solution.py:26
  128.4 8.5 %collective-permute-start.11 = (f32[7,32,4,1]{3,2,1,0:T(4,128)S(1)}, f32[7,32,4,1]{3,2,1,0:T(4,128)S(1)}, u32[]{:S(2)}, u32[]{:S(2)}) collective-permute-start(f32[7,32,4,1]{3,2,1,0:T(4,128)S(1)} %get-tuple-element.341), channel_id=1, source_target_pairs={{1,0},{2,1},{3,2},{0,3},{5,4},{6,5},{7,6},{4,7},{9,8},{10,9},{11,1... | collective-permute-start | bytes 10760 | tf_op jit(solution)/shard_map/ppermute | solution.py:28
  161.7 7.4 %collective-permute-start.12 = (f32[3,32,1,256]{3,2,1,0:T(1,128)S(1)}, f32[3,32,1,256]{3,2,1,0:T(1,128)S(1)}, u32[]{:S(2)}, u32[]{:S(2)}) collective-permute-start(f32[3,32,1,256]{3,2,1,0:T(1,128)S(1)} %get-tuple-element.467), channel_id=1, source_target_pairs={{0,4},{4,8},{8,12},{12,16},{16,20},{20,24},{24,28},{28,32},{32,36}... | collective-permute-start | bytes 294920 | tf_op jit(solution)/shard_map/ppermute | solution.py:26
  161.8 7.4 %collective-permute-start.13 = (f32[3,32,1,256]{3,2,1,0:T(1,128)S(1)}, f32[3,32,1,256]{3,2,1,0:T(1,128)S(1)}, u32[]{:S(2)}, u32[]{:S(2)}) collective-permute-start(f32[3,32,1,256]{3,2,1,0:T(1,128)S(1)} %get-tuple-element.468), channel_id=1, source_target_pairs={{4,0},{8,4},{12,8},{16,12},{20,16},{24,20},{28,24},{32,28},{36,32}... | collective-permute-start | bytes 294920 | tf_op jit(solution)/shard_map/ppermute | solution.py:28
  169.6 6.9 %collective-permute-start.14 = (f32[3,32,4,1]{3,2,1,0:T(4,128)S(1)}, f32[3,32,4,1]{3,2,1,0:T(4,128)S(1)}, u32[]{:S(2)}, u32[]{:S(2)}) collective-permute-start(f32[3,32,4,1]{3,2,1,0:T(4,128)S(1)} %get-tuple-element.432), channel_id=1, source_target_pairs={{0,1},{1,2},{2,3},{3,0},{4,5},{5,6},{6,7},{7,4},{8,9},{9,10},{10,1... | collective-permute-start | bytes 4616 | tf_op jit(solution)/shard_map/ppermute | solution.py:26
  171.3 5.7 %collective-permute-start.15 = (f32[3,32,4,1]{3,2,1,0:T(4,128)S(1)}, f32[3,32,4,1]{3,2,1,0:T(4,128)S(1)}, u32[]{:S(2)}, u32[]{:S(2)}) collective-permute-start(f32[3,32,4,1]{3,2,1,0:T(4,128)S(1)} %get-tuple-element.433), channel_id=1, source_target_pairs={{1,0},{2,1},{3,2},{0,3},{5,4},{6,5},{7,6},{4,7},{9,8},{10,9},{11,1... | collective-permute-start | bytes 4616 | tf_op jit(solution)/shard_map/ppermute | solution.py:28
  220.7 8.8 %collective-permute-start.16 = (f32[7,32,1,256]{3,2,1,0:T(1,128)S(1)}, f32[7,32,1,256]{3,2,1,0:T(1,128)S(1)}, u32[]{:S(2)}, u32[]{:S(2)}) collective-permute-start(f32[7,32,1,256]{3,2,1,0:T(1,128)S(1)} %get-tuple-element.416), channel_id=1, source_target_pairs={{0,4},{4,8},{8,12},{12,16},{16,20},{20,24},{24,28},{28,32},{32,36}... | collective-permute-start | bytes 688136 | tf_op jit(solution)/shard_map/ppermute | solution.py:26
  220.8 8.8 %collective-permute-start.17 = (f32[7,32,1,256]{3,2,1,0:T(1,128)S(1)}, f32[7,32,1,256]{3,2,1,0:T(1,128)S(1)}, u32[]{:S(2)}, u32[]{:S(2)}) collective-permute-start(f32[7,32,1,256]{3,2,1,0:T(1,128)S(1)} %get-tuple-element.417), channel_id=1, source_target_pairs={{4,0},{8,4},{12,8},{16,12},{20,16},{24,20},{28,24},{32,28},{36,32}... | collective-permute-start | bytes 688136 | tf_op jit(solution)/shard_map/ppermute | solution.py:28
  230.5 9.8 %collective-permute-start.18 = (f32[7,32,4,1]{3,2,1,0:T(4,128)S(1)}, f32[7,32,4,1]{3,2,1,0:T(4,128)S(1)}, u32[]{:S(2)}, u32[]{:S(2)}) collective-permute-start(f32[7,32,4,1]{3,2,1,0:T(4,128)S(1)} %get-tuple-element.322), channel_id=1, source_target_pairs={{0,1},{1,2},{2,3},{3,0},{4,5},{5,6},{6,7},{7,4},{8,9},{9,10},{10,1... | collective-permute-start | bytes 10760 | tf_op jit(solution)/shard_map/ppermute | solution.py:26
  232.0 8.5 %collective-permute-start.19 = (f32[7,32,4,1]{3,2,1,0:T(4,128)S(1)}, f32[7,32,4,1]{3,2,1,0:T(4,128)S(1)}, u32[]{:S(2)}, u32[]{:S(2)}) collective-permute-start(f32[7,32,4,1]{3,2,1,0:T(4,128)S(1)} %get-tuple-element.323), channel_id=1, source_target_pairs={{1,0},{2,1},{3,2},{0,3},{5,4},{6,5},{7,6},{4,7},{9,8},{10,9},{11,1... | collective-permute-start | bytes 10760 | tf_op jit(solution)/shard_map/ppermute | solution.py:28
  266.1 22.1 %collective-permute-start.20 = (f32[3,32,1,256]{3,2,1,0:T(1,128)}, f32[3,32,1,256]{3,2,1,0:T(1,128)S(1)}, u32[]{:S(2)}, u32[]{:S(2)}) collective-permute-start(f32[3,32,1,256]{3,2,1,0:T(1,128)} %get-tuple-element.459), channel_id=1, source_target_pairs={{0,4},{4,8},{8,12},{12,16},{16,20},{20,24},{24,28},{28,32},{32,36}... | collective-permute-start | bytes 294920 | tf_op jit(solution)/shard_map/ppermute | solution.py:26
  266.1 22.1 %collective-permute-start.21 = (f32[3,32,1,256]{3,2,1,0:T(1,128)}, f32[3,32,1,256]{3,2,1,0:T(1,128)S(1)}, u32[]{:S(2)}, u32[]{:S(2)}) collective-permute-start(f32[3,32,1,256]{3,2,1,0:T(1,128)} %get-tuple-element.460), channel_id=1, source_target_pairs={{4,0},{8,4},{12,8},{16,12},{20,16},{24,20},{28,24},{32,28},{36,32}... | collective-permute-start | bytes 294920 | tf_op jit(solution)/shard_map/ppermute | solution.py:28
  288.6 6.9 %collective-permute-start.22 = (f32[3,32,4,1]{3,2,1,0:T(4,128)S(1)}, f32[3,32,4,1]{3,2,1,0:T(4,128)S(1)}, u32[]{:S(2)}, u32[]{:S(2)}) collective-permute-start(f32[3,32,4,1]{3,2,1,0:T(4,128)S(1)} %get-tuple-element.428), channel_id=1, source_target_pairs={{0,1},{1,2},{2,3},{3,0},{4,5},{5,6},{6,7},{7,4},{8,9},{9,10},{10,1... | collective-permute-start | bytes 4616 | tf_op jit(solution)/shard_map/ppermute | solution.py:26
  290.2 5.7 %collective-permute-start.23 = (f32[3,32,4,1]{3,2,1,0:T(4,128)S(1)}, f32[3,32,4,1]{3,2,1,0:T(4,128)S(1)}, u32[]{:S(2)}, u32[]{:S(2)}) collective-permute-start(f32[3,32,4,1]{3,2,1,0:T(4,128)S(1)} %get-tuple-element.429), channel_id=1, source_target_pairs={{1,0},{2,1},{3,2},{0,3},{5,4},{6,5},{7,6},{4,7},{9,8},{10,9},{11,1... | collective-permute-start | bytes 4616 | tf_op jit(solution)/shard_map/ppermute | solution.py:28
  (88 other events, 762.1 us)
where the time goes:
time: 418 us; the launch traced here: 413 us
  other arithmetic  204 us (49%)
  local copies, waits for them, and re-layouts  104 us (25%)
  starting transfers between devices  52 us (12%)
  waiting for transfers between devices  36.5 us (9%)
  blocking collectives  13.5 us (3%)
    reduce_sum x9, other arithmetic, force_pair(): jnp.sum(strength * delta_x, axis=1)  118 us
    reduce_sum x9, other arithmetic, density_pair(): return jnp.sum(theirs[6][None, :] * weight, axis=1)  52.8 us
    scatter x1, local copies, waits for them, and re-layouts, shards(): jnp.zeros((8, sub_count * capacity), jnp.float32).at[:, flat_slot]  46 us
    ppermute x12, starting transfers between devices, with_halo(): lax.ppermute(head, axis, [((i + 1) % count, i) for i in range(count)])  42.3 us
    ppermute x12, waiting for transfers between devices, with_halo(): lax.ppermute(tail, axis, [(i, (i + 1) % count) for i in range(count)])  35.2 us
    concatenate x15, other arithmetic, with_halo(): jnp.concatenate([lax.ppermute(tail, axis, [(i, (i + 1) % count) for i in...  19.8 us
    sub x41, local copies, waits for them, and re-layouts, force_pair(): relative_x = local_part[3][:, None] - theirs[3][None, :]  16.8 us
    all_to_all x1, blocking collectives, shards(): lax.all_to_all(buffer, 'sub', split_axis=1, concat_axis=1, tiled=True)  13.5 us
  transfers between devices with their start and end apart: 24, of which 14 were waited for; matrix products, arithmetic and copies ran while one was open for 8% of the time, Pallas kernels for 0%

commit v1 on v0

v1 whole, which is shorter than its diff:
```python
import functools
import math

import jax
import jax.numpy as jnp
from jax import lax
from jax.experimental import pallas as pl
from jax.experimental.pallas import tpu as pltpu
from jax.sharding import PartitionSpec as P

MESH = pl.DeviceIdType.MESH

S = 32
LN = 128
KERNEL_NORM = 21.0 / (2.0 * math.pi)
NACT = (32, 16, 8)
NMOVED = (32, 32, 16)

X, Y, Z, VX, VY, VZ, MS, Q, C, R = range(10)
NF = 10


def field(row, comp, b, h):
    return ((row * NF + comp) * 3 + b) * 2 + h


def lane_iota():
    return lax.broadcasted_iota(jnp.int32, (8, LN), 1)


def stage_ids(stage, c):
    if stage == 0:
        return c // 2, 1 + c % 2, 1
    if stage == 1:
        return c // 4, 1 + (c // 2) % 2, 2 * (c % 2)
    return c // 3, 3 * (c // 3), c % 3


STAGE_SIZE = (4, 8, 6)
STAGE_BASE = (0, 4, 12)


def substeps_kernel(
    tiles, subs, off, vel, mass, ent, cnt, out, fld, st, pr, dens, acc, sq, ysend, xin, pin, yin,
    cache_w, cache_a, send_sem, recv_sem
):
    t, u = lax.axis_index("tile"), lax.axis_index("sub")
    up, down = lax.rem(t + 1, tiles), lax.rem(t + tiles - 1, tiles)
    right, left = lax.rem(u + 1, subs), lax.rem(u + subs - 1, subs)
    tile_of = (down, t, up)

    barrier = pltpu.get_barrier_semaphore()
    for dev in ((down, u), (up, u), (down, left), (t, left), (up, left), (down, right), (t, right), (up, right)):
        pl.semaphore_signal(barrier, inc=1, device_id=dev, device_id_type=MESH)

    for row in range(2):
        for h in range(2):
            count = jnp.broadcast_to(cnt[0, pl.ds(h * 2 + row, 1), :], (8, LN))
            for g in range(4):
                rows = pl.ds(g * 32 + h * 2 + row, 8, stride=4)
                dst = (row, h, pl.ds(g * 8, 8))
                for c in range(3):
                    st[(c,) + dst] = off[c, rows, :] * 4.0
                    st[(3 + c,) + dst] = vel[c, rows, :] * 16.0
                slot = lax.broadcasted_iota(jnp.int32, (8, LN), 0) + g * 8
                st[(6,) + dst] = jnp.where(slot < count, mass[rows, :] * (KERNEL_NORM / 64.0), 0.0)
                e = ent[rows, :]
                sq[(0,) + dst] = e
                sq[(1,) + dst] = jnp.sqrt(e * (5.0 / 3.0))
                pr[(2,) + dst] = jnp.full((8, LN), 4.0, jnp.float32)
    pl.semaphore_wait(barrier, 8)

    lane = lane_iota()

    def start_round(rnd, src, ncomp, n, inbox):
        for side in range(2):
            for g in range(n // 8):
                packed = jnp.zeros((8, LN), jnp.float32)
                for c in range(ncomp):
                    for row in range(2):
                        code = c * 2 + row
                        v = src[c, row, side, pl.ds(g * 8, 8), :]
                        from_lane = 127 if side == 1 else 0
                        v = pltpu.roll(v, (code - from_lane) % LN, 1)
                        packed = jnp.where(lane == code, v, packed)
                ysend[rnd, side, pl.ds(g * 8, 8), :] = packed
        copies = []
        for row, dst_t, slot in ((0, down, 1), (1, up, 0)):
            f = row
            copies.append(
                pltpu.make_async_remote_copy(
                    src_ref=src.at[pl.ds(0, ncomp), row, :, pl.ds(0, n)],
                    dst_ref=inbox.at[rnd // 2, slot, pl.ds(0, ncomp), :, pl.ds(0, n)],
                    send_sem=send_sem.at[rnd, f],
                    recv_sem=recv_sem.at[rnd, f],
                    device_id=(dst_t, u),
                    device_id_type=MESH,
                )
            )
        for dt in range(3):
            for side in range(2):
                f = 2 + dt * 2 + side
                copies.append(
                    pltpu.make_async_remote_copy(
                        src_ref=ysend.at[rnd, side, pl.ds(0, n)],
                        dst_ref=yin.at[rnd, 2 - dt, 1 - side, pl.ds(0, n)],
                        send_sem=send_sem.at[rnd, f],
                        recv_sem=recv_sem.at[rnd, f],
                        device_id=(tile_of[dt], right if side == 1 else left),
                        device_id_type=MESH,
                    )
                )
        for f in (4, 5, 0, 1, 2, 3, 6, 7):
            copies[f].start()
        return copies

    def shift_of(comp, r):
        return 4.0 * (r - 1) if comp == X else 0.0

    def centre(load, comps, r, n):
        for c, comp in enumerate(comps):
            for h in range(2):
                v = load(c, h, pl.ds(0, n))
                if comp == X and r != 1:
                    v = v + 4.0 * (r - 1)
                fld[field(r, comp, 1, h), pl.ds(0, n), :] = v

    def sides(load, comps, r, n, rnd, dt, sender_row):
        for c, comp in enumerate(comps):
            code = c * 2 + sender_row
            dx = 4.0 * (r - 1) if comp == X else 0.0
            for g in range(n // 8):
                rows = pl.ds(g * 8, 8)
                a0, a1 = load(c, 0, rows), load(c, 1, rows)
                lo = pltpu.roll(yin[rnd, dt, 0, rows, :], (0 - code) % LN, 1)
                hi = pltpu.roll(yin[rnd, dt, 1, rows, :], (127 - code) % LN, 1)
                r0, r1 = pltpu.roll(a0, 1, 1), pltpu.roll(a1, 1, 1)
                l0, l1 = pltpu.roll(a0, 127, 1), pltpu.roll(a1, 127, 1)
                first, last = lane == 0, lane == 127
                minus = [jnp.where(first, lo, r0), jnp.where(first, r0, r1)]
                plus = [jnp.where(last, l1, l0), jnp.where(last, hi, l1)]
                for h in range(2):
                    m, p = minus[h], plus[h]
                    if comp == Y:
                        m, p = m - 4.0, p + 4.0
                    elif comp == X and r != 1:
                        m, p = m + dx, p + dx
                    fld[field(r, comp, 0, h), rows, :] = m
                    fld[field(r, comp, 2, h), rows, :] = p

    def other(r, comp, b, h, j):
        return fld[field(r, comp, b, h), pl.ds(j, 8, stride=0), :]

    def own(row, comp, h, g, n):
        return fld[field(row + 1, comp, 1, h), pl.ds(g * 8, n * 8), :].reshape(n, 8, LN)

    def density_stage(stage, k):
        per = NACT[k] // 8
        unroll = (16, 16, 16)[k]
        base = STAGE_BASE[stage]

        def combo(ch, _):
            c, h = ch // 2, ch % 2
            row, r, b = stage_ids(stage, c)
            xi, yi, zi = (own(row, comp, h, 0, per) for comp in (X, Y, Z))
            slot = (base + c) * 2 + h
            total0 = dens[row, h, pl.ds(0, per * 8), :].reshape(per, 8, LN)

            def block(jb, total):
                for jj in range(unroll):
                    j = jb * unroll + jj
                    dx = xi - other(r, X, b, h, j)
                    dy = yi - other(r, Y, b, h, j)
                    dz = zi - other(r, Z, b, h, j)
                    r2 = dx * dx + dy * dy + dz * dz
                    rad = r2 * lax.rsqrt(jnp.maximum(r2, 1e-30))
                    s = jnp.maximum(4.0 - rad, 0.0)
                    w3 = (s * other(r, MS, b, h, j)) * (s * s)
                    total = total + w3 * (s * (5.0 - s))
                    at = slot * S + j
                    cache_w[at, pl.ds(0, per)] = w3
                    cache_a[at, pl.ds(0, per)] = r2 + 0.16
                return total

            total = lax.fori_loop(0, S // unroll, block, total0)
            dens[row, h, pl.ds(0, per * 8), :] = total.reshape(per * 8, LN)
            return 0

        lax.fori_loop(0, STAGE_SIZE[stage] * 2, combo, 0)

    def force_stage(stage, k):
        groups = NACT[k] // 8
        per = min(groups, 2)
        sets = groups // per
        unroll = (8, 8, 16)[k]
        base = STAGE_BASE[stage]

        def combo(chg, _):
            ch, g = chg // sets, (chg % sets) * per
            c, h = ch // 2, ch % 2
            row, r, b = stage_ids(stage, c)
            xi, yi, zi, vxi, vyi, vzi, qi, ci, ri = (
                own(row, comp, h, g, per) for comp in (X, Y, Z, VX, VY, VZ, Q, C, R)
            )
            slot = (base + c) * 2 + h
            total0 = tuple(acc[d, row, h, pl.ds(g * 8, per * 8), :].reshape(per, 8, LN) for d in range(3))

            def block(jb, total):
                ax, ay, az = total
                for jj in range(unroll):
                    j = jb * unroll + jj
                    at = slot * S + j
                    dx = xi - other(r, X, b, h, j)
                    dy = yi - other(r, Y, b, h, j)
                    dz = zi - other(r, Z, b, h, j)
                    n = (
                        dx * (vxi - other(r, VX, b, h, j))
                        + dy * (vyi - other(r, VY, b, h, j))
                        + dz * (vzi - other(r, VZ, b, h, j))
                    )
                    n = jnp.minimum(n, 0.0)
                    soft = cache_a[at, pl.ds(g, per)]
                    sound = ci + other(r, C, b, h, j)
                    rho = ri + other(r, R, b, h, j)
                    visc = (n * (n - sound * soft)) / ((soft * soft) * rho)
                    f = cache_w[at, pl.ds(g, per)] * (qi + other(r, Q, b, h, j) + visc)
                    ax, ay, az = ax + f * dx, ay + f * dy, az + f * dz
                return ax, ay, az

            total = lax.fori_loop(0, S // unroll, block, total0)
            for d in range(3):
                acc[d, row, h, pl.ds(g * 8, per * 8), :] = total[d].reshape(per * 8, LN)
            return 0

        lax.fori_loop(0, STAGE_SIZE[stage] * 2 * sets, combo, 0)

    def exchange_and_sum(rnd, src, inbox, comps, n, stage_fn, k):
        copies = start_round(rnd, src, len(comps), n, inbox)
        loads = [None] * 4
        for r in (1, 2):
            loads[r] = functools.partial(lambda row, c, h, rows: src[c, row, h, rows, :], r - 1)
        loads[0] = lambda c, h, rows: inbox[rnd // 2, 0, c, h, rows, :]
        loads[3] = lambda c, h, rows: inbox[rnd // 2, 1, c, h, rows, :]
        for r in (1, 2):
            centre(loads[r], comps, r, n)
        stage_fn(0, k)
        copies[4].wait_recv()
        copies[5].wait_recv()
        for r in (1, 2):
            sides(loads[r], comps, r, n, rnd, 1, r - 1)
        stage_fn(1, k)
        for f in (0, 1, 2, 3, 6, 7):
            copies[f].wait_recv()
        for r, dt, sender_row in ((0, 0, 1), (3, 2, 0)):
            centre(loads[r], comps, r, n)
            sides(loads[r], comps, r, n, rnd, dt, sender_row)
        stage_fn(2, k)
        return copies

    for k in range(3):
        n = NACT[k]
        dens[...] = jnp.zeros_like(dens)
        comps = (X, Y, Z, VX, VY, VZ) + ((MS,) if k == 0 else ())
        moved = exchange_and_sum(2 * k, st, xin, comps, NMOVED[k], density_stage, k)
        for row in range(2):
            for h in range(2):
                count = jnp.broadcast_to(cnt[k, pl.ds(h * 2 + row, 1), :], (8, LN))
                for g in range(n // 8):
                    rows = pl.ds(g * 8, 8)
                    slot = lax.broadcasted_iota(jnp.int32, (8, LN), 0) + g * 8
                    rho4 = jnp.where(slot < count, dens[row, h, rows, :], pr[2, row, h, rows, :])
                    root = jnp.exp(jnp.log(rho4 * 0.25) * (1.0 / 3.0))
                    pr[0, row, h, rows, :] = sq[0, row, h, rows, :] / root
                    pr[1, row, h, rows, :] = sq[1, row, h, rows, :] * root
                    pr[2, row, h, rows, :] = rho4
        acc[...] = jnp.zeros_like(acc)
        pressed = exchange_and_sum(2 * k + 1, pr, pin, (Q, C, R), n, force_stage, k)
        for copy in moved + pressed:
            copy.wait_send()
        for row in range(2):
            for h in range(2):
                count = jnp.broadcast_to(cnt[k, pl.ds(h * 2 + row, 1), :], (8, LN))
                for g in range(n // 8):
                    rows = pl.ds(g * 8, 8)
                    slot = lax.broadcasted_iota(jnp.int32, (8, LN), 0) + g * 8
                    active = slot < count
                    for d in range(3):
                        v = st[3 + d, row, h, rows, :]
                        x = st[d, row, h, rows, :]
                        v_new = v + 4.0 * acc[d, row, h, rows, :]
                        st[3 + d, row, h, rows, :] = jnp.where(active, v_new, v)
                        st[d, row, h, rows, :] = jnp.where(active, x + 0.0125 * v_new, x)

    for row in range(2):
        for h in range(2):
            count = jnp.broadcast_to(cnt[0, pl.ds(h * 2 + row, 1), :], (8, LN))
            for g in range(4):
                rows = pl.ds(g * 8, 8)
                slot = lax.broadcasted_iota(jnp.int32, (8, LN), 0) + g * 8
                in_rows = pl.ds(g * 32 + h * 2 + row, 8, stride=4)
                values = [st[d, row, h, rows, :] * 0.25 for d in range(3)]
                values += [st[3 + d, row, h, rows, :] * 0.0625 for d in range(3)]
                values += [pr[2, row, h, rows, :] * 0.25]
                values += [jnp.where(slot < count, mass[in_rows, :], 0.0)]
                for i, v in enumerate(values):
                    out[pl.ds(((g * 8) * 4 + row * 2 + h) * 8 + i, 8, stride=32), :] = v


def plan_kernel(targets, pos, table):
    tri_r = lax.broadcasted_iota(jnp.int32, (LN, LN), 0)
    tri_c = lax.broadcasted_iota(jnp.int32, (LN, LN), 1)
    before = (tri_r < tri_c).astype(jnp.bfloat16)
    ones = jnp.ones((LN, LN), jnp.bfloat16)
    order_r = (tri_r // 4) * 4 + (tri_r % 2) * 2 + (tri_r // 2) % 2
    order_c = (tri_c // 4) * 4 + (tri_c % 2) * 2 + (tri_c // 2) % 2
    earlier = (order_c < order_r).astype(jnp.bfloat16)
    dest = targets[...]
    start = jnp.zeros((LN, LN), jnp.float32)
    place = jnp.zeros((LN, LN), jnp.float32)
    info = jnp.zeros((LN, LN), jnp.float32)
    for d in range(4):
        mine = dest == d
        hot = jnp.where(mine, 1.0, 0.0).astype(jnp.bfloat16)
        inside = jnp.dot(hot, before, preferred_element_type=jnp.float32)
        counts = jnp.dot(hot, ones, preferred_element_type=jnp.float32)
        base = jnp.dot(earlier, counts.astype(jnp.bfloat16), preferred_element_type=jnp.float32)
        place = jnp.where(mine, start + inside, place)
        info = jnp.where(tri_c == d, base, info)
        info = jnp.where(tri_c == 4 + d, start, info)
        info = jnp.where(tri_c == 8 + d, counts, info)
        start = start + counts
    pos[...] = place.astype(jnp.int32)
    table[...] = info.astype(jnp.int32)


TILES = 48


def route_kernel(table, pos, state, out, order):
    row_q = lax.broadcasted_iota(jnp.int32, (LN, LN), 0)
    lane = lane_iota()
    unroll = 8

    def sort(i, _):
        for jj in range(unroll):
            ch = i * unroll + jj
            src = (ch // 4) * 4 + (ch % 2) * 2 + (ch // 2) % 2
            hot = jnp.where(row_q == jnp.broadcast_to(pos[pl.ds(src, 1), :], (LN, LN)), 1.0, 0.0).astype(jnp.bfloat16)
            v = state[pl.ds(ch * 8, 8), :]
            hi = v.astype(jnp.bfloat16)
            rest = v - hi.astype(jnp.float32)
            mid = rest.astype(jnp.bfloat16)
            low = (rest - mid.astype(jnp.float32)).astype(jnp.bfloat16)
            pieces = jnp.concatenate([hi, mid, low], axis=0)
            moved = lax.dot_general(pieces, hot, (((1,), (1,)), ((), ())), preferred_element_type=jnp.float32)
            order[ch] = (moved[0:8] + moved[8:16]) + moved[16:24]
        return 0

    out[...] = jnp.zeros_like(out)
    lax.fori_loop(0, LN // unroll, sort, 0)

    def lay(ch, _):
        src = (ch // 4) * 4 + (ch % 2) * 2 + (ch // 2) % 2
        v = order[ch]
        for d in range(4):
            base = table[src, d]
            start = table[src, 4 + d]
            count = table[src, 8 + d]
            w = base // LN
            skip = base - w * LN
            turned = pltpu.roll(v, lax.rem(skip - start + 2 * LN, LN), 1)
            keep = (lane >= skip) & (lane < skip + count)
            out[d, w] = jnp.where(keep, turned, out[d, w])
            out[d, w + 1] = jnp.where(lane < skip + count - LN, turned, out[d, w + 1])
        return 0

    lax.fori_loop(0, LN, lay, 0, unroll=2)


def exchange_kernel(subs, buf, out, local_sem, send_sem, recv_sem):
    t, u = lax.axis_index("tile"), lax.axis_index("sub")
    barrier = pltpu.get_barrier_semaphore()
    for k in range(1, subs):
        pl.semaphore_signal(barrier, inc=1, device_id=(t, lax.rem(u + k, subs)), device_id_type=MESH)
    pl.semaphore_wait(barrier, subs - 1)
    copies = []
    for k in (2, 1, 3):
        dst = lax.rem(u + k, subs)
        copy = pltpu.make_async_remote_copy(
            src_ref=buf.at[dst, pl.ds(0, TILES)],
            dst_ref=out.at[pl.ds(u * TILES, TILES)],
            send_sem=send_sem.at[k],
            recv_sem=recv_sem.at[k],
            device_id=(t, dst),
            device_id_type=MESH,
        )
        copy.start()
        copies.append(copy)
    mine = pltpu.make_async_copy(buf.at[u, pl.ds(0, TILES)], out.at[pl.ds(u * TILES, TILES)], local_sem)
    mine.start()
    mine.wait()
    for copy in copies:
        copy.wait_send()
    for copy in copies:
        copy.wait_recv()


def rows_of(a):
    lead = a.shape[:-2]
    a = a.reshape(lead + (2, 2, LN))
    a = jnp.swapaxes(a, -3, -2)
    return a


def shards(tiles, subs, offsets, velocity, mass, entropy, active_counts, targets):
    off = rows_of(offsets).reshape(3, LN, LN)
    vel = rows_of(velocity).reshape(3, LN, LN)
    mas = rows_of(mass).reshape(LN, LN)
    ent = rows_of(entropy).reshape(LN, LN)
    cnt = rows_of(active_counts).reshape(3, 4, LN)
    tgt = rows_of(targets).reshape(LN, LN)
    vmem = pl.BlockSpec(memory_space=pltpu.VMEM)
    f32 = jnp.float32
    pos, table = pl.pallas_call(
        plan_kernel,
        out_shape=[jax.ShapeDtypeStruct((LN, LN), jnp.int32)] * 2,
        in_specs=[vmem],
        out_specs=[vmem] * 2,
        name="plan",
    )(tgt)
    state = pl.pallas_call(
        functools.partial(substeps_kernel, tiles, subs),
        out_shape=jax.ShapeDtypeStruct((8 * LN, LN), f32),
        in_specs=[vmem] * 5,
        out_specs=vmem,
        scratch_shapes=[
            pltpu.VMEM((4 * NF * 6, S, LN), f32),
            pltpu.VMEM((7, 2, 2, S, LN), f32),
            pltpu.VMEM((3, 2, 2, S, LN), f32),
            pltpu.VMEM((2, 2, S, LN), f32),
            pltpu.VMEM((3, 2, 2, S, LN), f32),
            pltpu.VMEM((2, 2, 2, S, LN), f32),
            pltpu.VMEM((6, 2, S, LN), f32),
            pltpu.VMEM((3, 2, 7, 2, S, LN), f32),
            pltpu.VMEM((3, 2, 3, 2, S, LN), f32),
            pltpu.VMEM((6, 3, 2, S, LN), f32),
            pltpu.VMEM((18 * 2 * S, 4, 8, LN), f32),
            pltpu.VMEM((18 * 2 * S, 4, 8, LN), f32),
            pltpu.SemaphoreType.DMA((6, 8)),
            pltpu.SemaphoreType.DMA((6, 8)),
        ],
        compiler_params=pltpu.CompilerParams(collective_id=0, has_side_effects=True, vmem_limit_bytes=62 * 1024 * 1024),
        name="substeps",
    )(off, vel, mas, ent, cnt)
    buf = pl.pallas_call(
        route_kernel,
        out_shape=jax.ShapeDtypeStruct((subs, TILES + 2, 8, LN), f32),
        in_specs=[pl.BlockSpec(memory_space=pltpu.SMEM), vmem, vmem],
        out_specs=vmem,
        scratch_shapes=[pltpu.VMEM((LN, 8, LN), f32)],
        name="route",
    )(table, pos, state)
    arrived = pl.pallas_call(
        functools.partial(exchange_kernel, subs),
        out_shape=jax.ShapeDtypeStruct((subs * TILES, 8, LN), f32),
        in_specs=[vmem],
        out_specs=vmem,
        scratch_shapes=[pltpu.SemaphoreType.DMA, pltpu.SemaphoreType.DMA((4,)), pltpu.SemaphoreType.DMA((4,))],
        compiler_params=pltpu.CompilerParams(collective_id=1, has_side_effects=True),
        name="exchange",
    )(buf)
    return jnp.transpose(arrived, (1, 0, 2)).reshape(8, subs * TILES * LN)


def solution(mesh):
    tiles, subs = mesh.shape["tile"], mesh.shape["sub"]
    placed = (
        P(None, None, "tile", "sub"),
        P(None, None, "tile", "sub"),
        P(None, "tile", "sub"),
        P(None, "tile", "sub"),
        P(None, "tile", "sub"),
        P(None, "tile", "sub"),
    )
    return jax.shard_map(
        functools.partial(shards, tiles, subs),
        mesh=mesh,
        in_specs=placed,
        out_specs=P(None, ("tile", "sub")),
        check_vma=False,
    )
```

time: 418 us -> 123 us (0.29); the launches traced: 413 us -> 123 us
  other arithmetic: 204 us -> 0 us
  Pallas kernels: 0 us -> 121 us
  local copies, waits for them, and re-layouts: 104 us -> 2.06 us
  starting transfers between devices: 52 us -> 0 us
  waiting for transfers between devices: 36.5 us -> 0 us
  blocking collectives: 13.5 us -> 0 us
    reduce_sum x19 -> x0, other arithmetic: 171 us -> none  [the longest x9 118 us: force_pair(): jnp.sum(strength * delta_x, axis=1)]
    pallas_call x0 -> x4, Pallas kernels: none -> 121 us  [the longest x1 90.8 us: shards(): pl.pallas_call(functools.partial(substeps_kernel, tiles, subs), out_shape...]
    ppermute x24 -> x0, starting transfers between devices: 52 us -> none  [the longest x12 42.3 us: with_halo(): lax.ppermute(head, axis, [((i + 1) % count, i) for i in range(count)])]
    scatter x1 -> x0, local copies, waits for them, and re-layouts: 46 us -> none  [shards(): jnp.zeros((8, sub_count * capacity), jnp.float32).at[:, flat_slot]]
    ppermute x24 -> x0, waiting for transfers between devices: 36.5 us -> none  [the longest x12 35.2 us: with_halo(): lax.ppermute(tail, axis, [(i, (i + 1) % count) for i in range(count)])]
    sub x179 -> x0, local copies, waits for them, and re-layouts: 31 us -> none  [the longest x41 16.8 us: force_pair(): relative_x = local_part[3][:, None] - theirs[3][None, :]]
    concatenate x19 -> x0, other arithmetic: 21.8 us -> none  [the longest x15 19.8 us: with_halo(): jnp.concatenate([lax.ppermute(tail, axis, [(i, (i + 1) % count) for i in...]
    all_to_all x1 -> x0, blocking collectives: 13.5 us -> none  [shards(): lax.all_to_all(buffer, 'sub', split_axis=1, concat_axis=1, tiled=True)]
  transfers between devices with their start and end apart: 24 -> 0, of which waited for: 14 -> 0; matrix products, arithmetic and copies ran while one was open for 8% -> 0% of each run, Pallas kernels for 0% -> 0%
where the time goes in v1:
time: 123 us
  Pallas kernels  121 us (98%)
  local copies, waits for them, and re-layouts  2.06 us (2%)
    pallas_call x1, Pallas kernels, shards(): pl.pallas_call(functools.partial(substeps_kernel, tiles, subs), out_shape...  90.8 us
    pallas_call x1, Pallas kernels, shards(): pl.pallas_call(route_kernel, out_shape=jax.ShapeDtypeStruct((subs, TILES...  16 us
    pallas_call x1, Pallas kernels, shards(): pl.pallas_call(functools.partial(exchange_kernel, subs), out_shape=jax.Sh...  11.6 us

profile of v1, /device:TPU:0, one launch (start us, length us, event | category | flops | bytes accessed | tf_op | source)
XLA Modules:
  0.0 122.6 jit_solution(3402539659323484050)
XLA Ops:
  0.0 2.1 %plan.1 = (s32[128,128]{1,0:T(8,128)}, s32[128,128]{1,0:T(8,128)}) custom-call(s32[128,128]{1,0:T(8,128)} %bitcast.38), custom_call_target="tpu_custom_call" | custom-call | tf_op jit(solution)/shard_map/plan/pallas_call | solution.py:424
  2.1 90.8 %substeps.1.state = f32[1024,128]{1,0:T(8,128)} custom-call(f32[3,128,128]{2,1,0:T(8,128)} %bitcast.34, f32[3,128,128]{2,1,0:T(8,128)} %bitcast.35, f32[128,128]{1,0:T(8,128)} %bitcast.36, f32[128,128]{1,0:T(8,128)} %bitcast.37, s32[3,4,128]{2,1,0:T(4,128)} %bitcast.39), custom_call_target="tpu_custom_call" | custom-call | tf_op jit(solution)/shard_map/substeps/pallas_call | solution.py:431
  92.9 16.0 %route.1.buf = f32[4,50,8,128]{3,2,1,0:T(8,128)} custom-call(s32[128,128]{1,0:T(8,128)} %get-tuple-element.7.table, s32[128,128]{1,0:T(8,128)} %get-tuple-element.8.pos, f32[1024,128]{1,0:T(8,128)} %substeps.1.state), custom_call_target="tpu_custom_call" | custom-call | tf_op jit(solution)/shard_map/route/pallas_call | solution.py:455
  108.9 11.6 %exchange.1 = f32[192,8,128]{2,1,0:T(8,128)} custom-call(f32[4,50,8,128]{3,2,1,0:T(8,128)} %route.1.buf), custom_call_target="tpu_custom_call" | custom-call | tf_op jit(solution)/shard_map/exchange/pallas_call | solution.py:463
  120.5 2.1 %copy.14 = f32[8,24576]{1,0:T(8,128)} copy(f32[8,24576]{1,0:T(8,128)} %bitcast.33) | data formatting | bytes 1572864

commit v2 on v1

--- a/solution.py
+++ b/solution.py
@@ -156,83 +156,78 @@
 
     def density_stage(stage, k):
         per = NACT[k] // 8
-        unroll = (16, 16, 16)[k]
+        halves = 2 if per == 1 else 1
         base = STAGE_BASE[stage]
 
-        def combo(ch, _):
-            c, h = ch // 2, ch % 2
+        def pairs(c, h):
             row, r, b = stage_ids(stage, c)
             xi, yi, zi = (own(row, comp, h, 0, per) for comp in (X, Y, Z))
             slot = (base + c) * 2 + h
-            total0 = dens[row, h, pl.ds(0, per * 8), :].reshape(per, 8, LN)
-
-            def block(jb, total):
-                for jj in range(unroll):
-                    j = jb * unroll + jj
-                    dx = xi - other(r, X, b, h, j)
-                    dy = yi - other(r, Y, b, h, j)
-                    dz = zi - other(r, Z, b, h, j)
-                    r2 = dx * dx + dy * dy + dz * dz
-                    rad = r2 * lax.rsqrt(jnp.maximum(r2, 1e-30))
-                    s = jnp.maximum(4.0 - rad, 0.0)
-                    w3 = (s * other(r, MS, b, h, j)) * (s * s)
-                    total = total + w3 * (s * (5.0 - s))
-                    at = slot * S + j
-                    cache_w[at, pl.ds(0, per)] = w3
-                    cache_a[at, pl.ds(0, per)] = r2 + 0.16
-                return total
-
-            total = lax.fori_loop(0, S // unroll, block, total0)
+            total = dens[row, h, pl.ds(0, per * 8), :].reshape(per, 8, LN)
+            for j in range(S):
+                dx = xi - other(r, X, b, h, j)
+                dy = yi - other(r, Y, b, h, j)
+                dz = zi - other(r, Z, b, h, j)
+                r2 = dx * dx + dy * dy + dz * dz
+                rad = r2 * lax.rsqrt(jnp.maximum(r2, 1e-30))
+                s = jnp.maximum(4.0 - rad, 0.0)
+                w3 = (s * other(r, MS, b, h, j)) * (s * s)
+                total = total + w3 * (s * (5.0 - s))
+                cache_w[slot * S + j, pl.ds(0, per)] = w3
+                cache_a[slot * S + j, pl.ds(0, per)] = 1.0 / (r2 + 0.16)
             dens[row, h, pl.ds(0, per * 8), :] = total.reshape(per * 8, LN)
+
+        def combo(i, _):
+            if halves == 2:
+                pairs(i, 0)
+                pairs(i, 1)
+            else:
+                pairs(i // 2, i % 2)
             return 0
 
-        lax.fori_loop(0, STAGE_SIZE[stage] * 2, combo, 0)
+        lax.fori_loop(0, STAGE_SIZE[stage] * 2 // halves, combo, 0)
 
     def force_stage(stage, k):
         groups = NACT[k] // 8
         per = min(groups, 2)
         sets = groups // per
-        unroll = (8, 8, 16)[k]
+        halves = 2 if per == 1 else 1
         base = STAGE_BASE[stage]
 
-        def combo(chg, _):
-            ch, g = chg // sets, (chg % sets) * per
-            c, h = ch // 2, ch % 2
+        def pairs(c, h, g):
             row, r, b = stage_ids(stage, c)
             xi, yi, zi, vxi, vyi, vzi, qi, ci, ri = (
                 own(row, comp, h, g, per) for comp in (X, Y, Z, VX, VY, VZ, Q, C, R)
             )
             slot = (base + c) * 2 + h
-            total0 = tuple(acc[d, row, h, pl.ds(g * 8, per * 8), :].reshape(per, 8, LN) for d in range(3))
-
-            def block(jb, total):
-                ax, ay, az = total
-                for jj in range(unroll):
-                    j = jb * unroll + jj
-                    at = slot * S + j
-                    dx = xi - other(r, X, b, h, j)
-                    dy = yi - other(r, Y, b, h, j)
-                    dz = zi - other(r, Z, b, h, j)
-                    n = (
-                        dx * (vxi - other(r, VX, b, h, j))
-                        + dy * (vyi - other(r, VY, b, h, j))
-                        + dz * (vzi - other(r, VZ, b, h, j))
-                    )
-                    n = jnp.minimum(n, 0.0)
-                    soft = cache_a[at, pl.ds(g, per)]
-                    sound = ci + other(r, C, b, h, j)
-                    rho = ri + other(r, R, b, h, j)
-                    visc = (n * (n - sound * soft)) / ((soft * soft) * rho)
-                    f = cache_w[at, pl.ds(g, per)] * (qi + other(r, Q, b, h, j) + visc)
-                    ax, ay, az = ax + f * dx, ay + f * dy, az + f * dz
-                return ax, ay, az
-
-            total = lax.fori_loop(0, S // unroll, block, total0)
-            for d in range(3):
-                acc[d, row, h, pl.ds(g * 8, per * 8), :] = total[d].reshape(per * 8, LN)
+            ax, ay, az = (acc[d, row, h, pl.ds(g * 8, per * 8), :].reshape(per, 8, LN) for d in range(3))
+            for j in range(S):
+                dx = xi - other(r, X, b, h, j)
+                dy = yi - other(r, Y, b, h, j)
+                dz = zi - other(r, Z, b, h, j)
+                n = (
+                    dx * (vxi - other(r, VX, b, h, j))
+                    + dy * (vyi - other(r, VY, b, h, j))
+                    + dz * (vzi - other(r, VZ, b, h, j))
+                )
+                mu = jnp.minimum(n, 0.0) * cache_a[slot * S + j, pl.ds(g, per)]
+                sound = ci + other(r, C, b, h, j)
+                visc = (mu * (mu - sound)) / (ri + other(r, R, b, h, j))
+                f = cache_w[slot * S + j, pl.ds(g, per)] * (qi + other(r, Q, b, h, j) + visc)
+                ax, ay, az = ax + f * dx, ay + f * dy, az + f * dz
+            for d, total in enumerate((ax, ay, az)):
+                acc[d, row, h, pl.ds(g * 8, per * 8), :] = total.reshape(per * 8, LN)
+
+        def combo(i, _):
+            if halves == 2:
+                pairs(i, 0, 0)
+                pairs(i, 1, 0)
+            else:
+                ch, g = i // sets, (i % sets) * per
+                pairs(ch // 2, ch % 2, g)
             return 0
 
-        lax.fori_loop(0, STAGE_SIZE[stage] * 2 * sets, combo, 0)
+        lax.fori_loop(0, STAGE_SIZE[stage] * 2 * sets // halves, combo, 0)
 
     def exchange_and_sum(rnd, src, inbox, comps, n, stage_fn, k):
         copies = start_round(rnd, src, len(comps), n, inbox)

time: 123 us -> 119 us (0.967)
  Pallas kernels: 121 us -> 116 us
    pallas_call x1, Pallas kernels: 90.8 us -> 85.8 us  [shards(): pl.pallas_call(functools.partial(substeps_kernel, tiles, subs), out_shape...]
where the time goes in v2:
time: 119 us; the launch traced here: 118 us
  Pallas kernels  116 us (97%)
  local copies, waits for them, and re-layouts  2.06 us (2%)
    pallas_call x1, Pallas kernels, shards(): pl.pallas_call(functools.partial(substeps_kernel, tiles, subs), out_shape...  85.8 us
    pallas_call x1, Pallas kernels, shards(): pl.pallas_call(route_kernel, out_shape=jax.ShapeDtypeStruct((subs, TILES...  16 us
    pallas_call x1, Pallas kernels, shards(): pl.pallas_call(functools.partial(exchange_kernel, subs), out_shape=jax.Sh...  12.3 us

profile of v2, /device:TPU:0, one launch (start us, length us, event | category | flops | bytes accessed | tf_op | source)
XLA Modules:
  0.0 118.3 jit_solution(11459447787266869200)
XLA Ops:
  0.0 2.1 %plan.1 = (s32[128,128]{1,0:T(8,128)}, s32[128,128]{1,0:T(8,128)}) custom-call(s32[128,128]{1,0:T(8,128)} %bitcast.38), custom_call_target="tpu_custom_call" | custom-call | tf_op jit(solution)/shard_map/plan/pallas_call | solution.py:419
  2.1 85.8 %substeps.1.state = f32[1024,128]{1,0:T(8,128)} custom-call(f32[3,128,128]{2,1,0:T(8,128)} %bitcast.34, f32[3,128,128]{2,1,0:T(8,128)} %bitcast.35, f32[128,128]{1,0:T(8,128)} %bitcast.36, f32[128,128]{1,0:T(8,128)} %bitcast.37, s32[3,4,128]{2,1,0:T(4,128)} %bitcast.39), custom_call_target="tpu_custom_call" | custom-call | tf_op jit(solution)/shard_map/substeps/pallas_call | solution.py:426
  87.9 16.0 %route.1.buf = f32[4,50,8,128]{3,2,1,0:T(8,128)} custom-call(s32[128,128]{1,0:T(8,128)} %get-tuple-element.7.table, s32[128,128]{1,0:T(8,128)} %get-tuple-element.8.pos, f32[1024,128]{1,0:T(8,128)} %substeps.1.state), custom_call_target="tpu_custom_call" | custom-call | tf_op jit(solution)/shard_map/route/pallas_call | solution.py:450
  103.9 12.3 %exchange.1 = f32[192,8,128]{2,1,0:T(8,128)} custom-call(f32[4,50,8,128]{3,2,1,0:T(8,128)} %route.1.buf), custom_call_target="tpu_custom_call" | custom-call | tf_op jit(solution)/shard_map/exchange/pallas_call | solution.py:458
  116.2 2.1 %copy.14 = f32[8,24576]{1,0:T(8,128)} copy(f32[8,24576]{1,0:T(8,128)} %bitcast.33) | data formatting | bytes 1572864

commit v3 on v2

--- a/solution.py
+++ b/solution.py
@@ -41,8 +41,8 @@
 
 
 def substeps_kernel(
-    tiles, subs, off, vel, mass, ent, cnt, out, fld, st, pr, dens, acc, sq, ysend, xin, pin, yin,
-    cache_w, cache_a, send_sem, recv_sem
+    tiles, subs, off, vel, mass, ent, cnt, tgt, gathered, runs, fld, st, pr, dens, acc, sq, ysend, xin, pin, yin,
+    cache_w, cache_a, raw, pos, tab, send_sem, recv_sem, tab_send, tab_recv, piece_send, piece_recv
 ):
     t, u = lax.axis_index("tile"), lax.axis_index("sub")
     up, down = lax.rem(t + 1, tiles), lax.rem(t + tiles - 1, tiles)
@@ -50,7 +50,9 @@
     tile_of = (down, t, up)
 
     barrier = pltpu.get_barrier_semaphore()
-    for dev in ((down, u), (up, u), (down, left), (t, left), (up, left), (down, right), (t, right), (up, right)):
+    across = lax.rem(u + 2, subs)
+    near = ((down, u), (up, u), (down, left), (t, left), (up, left), (down, right), (t, right), (up, right))
+    for dev in near + ((t, across),):
         pl.semaphore_signal(barrier, inc=1, device_id=dev, device_id_type=MESH)
 
     for row in range(2):
@@ -68,7 +70,7 @@
                 sq[(0,) + dst] = e
                 sq[(1,) + dst] = jnp.sqrt(e * (5.0 / 3.0))
                 pr[(2,) + dst] = jnp.full((8, LN), 4.0, jnp.float32)
-    pl.semaphore_wait(barrier, 8)
+    pl.semaphore_wait(barrier, 9)
 
     lane = lane_iota()
 
@@ -229,8 +231,119 @@
 
         lax.fori_loop(0, STAGE_SIZE[stage] * 2 * sets // halves, combo, 0)
 
-    def exchange_and_sum(rnd, src, inbox, comps, n, stage_fn, k):
+    def plan():
+        row_i = lax.broadcasted_iota(jnp.int32, (LN, LN), 0)
+        col_i = lax.broadcasted_iota(jnp.int32, (LN, LN), 1)
+        before = jnp.where(row_i < col_i, 1.0, 0.0).astype(jnp.bfloat16)
+        ones = jnp.ones((LN, LN), jnp.bfloat16)
+        row8 = lax.broadcasted_iota(jnp.int32, (8, LN), 0)
+        dest = tgt[...]
+        start = jnp.zeros((LN, LN), jnp.float32)
+        place = jnp.zeros((LN, LN), jnp.float32)
+        start_t = jnp.zeros((8, LN), jnp.float32)
+        info = jnp.zeros((8, LN), jnp.float32)
+        for d in range(subs):
+            mine = dest == d
+            hot = jnp.where(mine, 1.0, 0.0).astype(jnp.bfloat16)
+            inside = jnp.dot(hot, before, preferred_element_type=jnp.float32)
+            place = jnp.where(mine, start + inside, place)
+            start = start + jnp.dot(hot, ones, preferred_element_type=jnp.float32)
+            count_t = lax.dot_general(
+                ones[0:8], hot, (((1,), (1,)), ((), ())), preferred_element_type=jnp.float32
+            )
+            info = jnp.where(row8 == d, start_t, info)
+            info = jnp.where(row8 == subs + d, count_t, info)
+            start_t = start_t + count_t
+        pos[...] = place.astype(jnp.int32)
+        tab[u] = info
+        sends = []
+        for k in range(1, subs):
+            copy = pltpu.make_async_remote_copy(
+                src_ref=tab.at[u],
+                dst_ref=tab.at[u],
+                send_sem=tab_send.at[k],
+                recv_sem=tab_recv.at[k],
+                device_id=(t, lax.rem(u + k, subs)),
+                device_id_type=MESH,
+            )
+            copy.start()
+            sends.append(copy)
+        return sends
+
+    def emit(g):
+        row_q = lax.broadcasted_iota(jnp.int32, (LN, LN), 0)
+        for row in range(2):
+            for h in range(2):
+                count = jnp.broadcast_to(cnt[0, pl.ds(h * 2 + row, 1), :], (8, LN))
+                rows = pl.ds(g * 8, 8)
+                slot = lax.broadcasted_iota(jnp.int32, (8, LN), 0) + g * 8
+                in_rows = pl.ds(g * 32 + h * 2 + row, 8, stride=4)
+                values = [st[d, row, h, rows, :] * 0.25 for d in range(3)]
+                values += [st[3 + d, row, h, rows, :] * 0.0625 for d in range(3)]
+                values += [pr[2, row, h, rows, :] * 0.25]
+                values += [jnp.where(slot < count, mass[in_rows, :], 0.0)]
+                for i, v in enumerate(values):
+                    raw[g, pl.ds((h * 2 + row) * 64 + i, 8, stride=8), :] = v
+
+        def sort(hr, _):
+            for i in range(8):
+                at = (g * 8 + i) * 4 + hr
+                hot = jnp.where(row_q == jnp.broadcast_to(pos[pl.ds(at, 1), :], (LN, LN)), 1.0, 0.0)
+                v = raw[g, pl.ds(hr * 64 + i * 8, 8), :]
+                hi = v.astype(jnp.bfloat16)
+                rest = v - hi.astype(jnp.float32)
+                mid = rest.astype(jnp.bfloat16)
+                low = (rest - mid.astype(jnp.float32)).astype(jnp.bfloat16)
+                pieces = jnp.concatenate([hi, mid, low], axis=0)
+                moved = lax.dot_general(
+                    pieces, hot.astype(jnp.bfloat16), (((1,), (1,)), ((), ())), preferred_element_type=jnp.float32
+                )
+                gathered[u, at] = (moved[0:8] + moved[8:16]) + moved[16:24]
+            return 0
+
+        lax.fori_loop(0, 4, sort, 0)
+
+    PIECES = ((64, 64), (32, 32), (0, 32))
+
+    def piece_copy(p, flow, owner, first, rows, dst):
+        return pltpu.make_async_remote_copy(
+            src_ref=gathered.at[owner, pl.ds(first, rows)],
+            dst_ref=gathered.at[owner, pl.ds(first, rows)],
+            send_sem=piece_send.at[p, flow],
+            recv_sem=piece_recv.at[p, flow],
+            device_id=(t, dst),
+            device_id_type=MESH,
+        )
+
+    def start_piece(p):
+        first, rows = PIECES[p]
+        for g in range(first // 32, (first + rows) // 32):
+            emit(g)
+        half = rows // 2
+        copies = [
+            piece_copy(p, 0, u, first, half, right),
+            piece_copy(p, 1, u, first + half, half, right),
+            piece_copy(p, 2, u, first + half, half, left),
+            piece_copy(p, 3, u, first, half, left),
+        ]
+        for f in (0, 2, 1, 3):
+            copies[f].start()
+        return copies
+
+    def forward_piece(p):
+        first, rows = PIECES[p]
+        half = rows // 2
+        copies = [
+            piece_copy(p, 4, left, first, half, right),
+            piece_copy(p, 5, right, first + half, half, left),
+        ]
+        for copy in copies:
+            copy.start()
+        return copies
+
+    def exchange_and_sum(rnd, src, inbox, comps, n, stage_fn, k, meanwhile):
         copies = start_round(rnd, src, len(comps), n, inbox)
+        meanwhile()
         loads = [None] * 4
         for r in (1, 2):
             loads[r] = functools.partial(lambda row, c, h, rows: src[c, row, h, rows, :], r - 1)
@@ -252,11 +365,26 @@
         stage_fn(2, k)
         return copies
 
+    pending = []
+    arriving = {}
+
+    def during(rnd):
+        if rnd == 0:
+            arriving["tab"] = plan()
+        elif rnd in (2, 4):
+            arriving[rnd] = start_piece(rnd // 2 - 1)
+        elif rnd in (3, 5):
+            p = rnd // 2 - 1
+            copies = arriving[rnd - 1]
+            copies[0].wait_recv()
+            copies[2].wait_recv()
+            arriving[rnd] = forward_piece(p)
+
     for k in range(3):
         n = NACT[k]
         dens[...] = jnp.zeros_like(dens)
         comps = (X, Y, Z, VX, VY, VZ) + ((MS,) if k == 0 else ())
-        moved = exchange_and_sum(2 * k, st, xin, comps, NMOVED[k], density_stage, k)
+        moved = exchange_and_sum(2 * k, st, xin, comps, NMOVED[k], density_stage, k, lambda: during(2 * k))
         for row in range(2):
             for h in range(2):
                 count = jnp.broadcast_to(cnt[k, pl.ds(h * 2 + row, 1), :], (8, LN))
@@ -269,7 +397,7 @@
                     pr[1, row, h, rows, :] = sq[1, row, h, rows, :] * root
                     pr[2, row, h, rows, :] = rho4
         acc[...] = jnp.zeros_like(acc)
-        pressed = exchange_and_sum(2 * k + 1, pr, pin, (Q, C, R), n, force_stage, k)
+        pressed = exchange_and_sum(2 * k + 1, pr, pin, (Q, C, R), n, force_stage, k, lambda: during(2 * k + 1))
         for copy in moved + pressed:
             copy.wait_send()
         for row in range(2):
@@ -285,119 +413,63 @@
                         v_new = v + 4.0 * acc[d, row, h, rows, :]
                         st[3 + d, row, h, rows, :] = jnp.where(active, v_new, v)
                         st[d, row, h, rows, :] = jnp.where(active, x + 0.0125 * v_new, x)
-
-    for row in range(2):
-        for h in range(2):
-            count = jnp.broadcast_to(cnt[0, pl.ds(h * 2 + row, 1), :], (8, LN))
-            for g in range(4):
-                rows = pl.ds(g * 8, 8)
-                slot = lax.broadcasted_iota(jnp.int32, (8, LN), 0) + g * 8
-                in_rows = pl.ds(g * 32 + h * 2 + row, 8, stride=4)
-                values = [st[d, row, h, rows, :] * 0.25 for d in range(3)]
-                values += [st[3 + d, row, h, rows, :] * 0.0625 for d in range(3)]
-                values += [pr[2, row, h, rows, :] * 0.25]
-                values += [jnp.where(slot < count, mass[in_rows, :], 0.0)]
-                for i, v in enumerate(values):
-                    out[pl.ds(((g * 8) * 4 + row * 2 + h) * 8 + i, 8, stride=32), :] = v
-
-
-def plan_kernel(targets, pos, table):
-    tri_r = lax.broadcasted_iota(jnp.int32, (LN, LN), 0)
-    tri_c = lax.broadcasted_iota(jnp.int32, (LN, LN), 1)
-    before = (tri_r < tri_c).astype(jnp.bfloat16)
-    ones = jnp.ones((LN, LN), jnp.bfloat16)
-    order_r = (tri_r // 4) * 4 + (tri_r % 2) * 2 + (tri_r // 2) % 2
-    order_c = (tri_c // 4) * 4 + (tri_c % 2) * 2 + (tri_c // 2) % 2
-    earlier = (order_c < order_r).astype(jnp.bfloat16)
-    dest = targets[...]
-    start = jnp.zeros((LN, LN), jnp.float32)
-    place = jnp.zeros((LN, LN), jnp.float32)
-    info = jnp.zeros((LN, LN), jnp.float32)
-    for d in range(4):
-        mine = dest == d
-        hot = jnp.where(mine, 1.0, 0.0).astype(jnp.bfloat16)
-        inside = jnp.dot(hot, before, preferred_element_type=jnp.float32)
-        counts = jnp.dot(hot, ones, preferred_element_type=jnp.float32)
-        base = jnp.dot(earlier, counts.astype(jnp.bfloat16), preferred_element_type=jnp.float32)
-        place = jnp.where(mine, start + inside, place)
-        info = jnp.where(tri_c == d, base, info)
-        info = jnp.where(tri_c == 4 + d, start, info)
-        info = jnp.where(tri_c == 8 + d, counts, info)
-        start = start + counts
-    pos[...] = place.astype(jnp.int32)
-    table[...] = info.astype(jnp.int32)
+    for rnd in (3, 5):
+        direct, passed = arriving[rnd - 1], arriving[rnd]
+        pending += direct + passed
+        for copy in (direct[1], direct[3], passed[0], passed[1]):
+            copy.wait_recv()
+    pending += arriving["tab"]
+    for copy in arriving["tab"]:
+        copy.wait_recv()
+
+
+    copies = start_piece(2)
+    copies[0].wait_recv()
+    copies[2].wait_recv()
+    forward = forward_piece(2)
+    pending += copies + forward
+    for src in range(subs):
+        runs[src : src + 1, :] = tab[src, pl.ds(u, 1), :].astype(jnp.int32)
+        runs[subs + src : subs + src + 1, :] = tab[src, pl.ds(subs + u, 1), :].astype(jnp.int32)
+    for copy in pending:
+        copy.wait_send()
+    for copy in (copies[1], copies[3], forward[0], forward[1]):
+        copy.wait_recv()
 
 
 TILES = 48
 
 
-def route_kernel(table, pos, state, out, order):
-    row_q = lax.broadcasted_iota(jnp.int32, (LN, LN), 0)
+def lay_kernel(runs, gathered, out, tiles):
+    subs = gathered.shape[0]
     lane = lane_iota()
-    unroll = 8
-
-    def sort(i, _):
-        for jj in range(unroll):
-            ch = i * unroll + jj
-            src = (ch // 4) * 4 + (ch % 2) * 2 + (ch // 2) % 2
-            hot = jnp.where(row_q == jnp.broadcast_to(pos[pl.ds(src, 1), :], (LN, LN)), 1.0, 0.0).astype(jnp.bfloat16)
-            v = state[pl.ds(ch * 8, 8), :]
-            hi = v.astype(jnp.bfloat16)
-            rest = v - hi.astype(jnp.float32)
-            mid = rest.astype(jnp.bfloat16)
-            low = (rest - mid.astype(jnp.float32)).astype(jnp.bfloat16)
-            pieces = jnp.concatenate([hi, mid, low], axis=0)
-            moved = lax.dot_general(pieces, hot, (((1,), (1,)), ((), ())), preferred_element_type=jnp.float32)
-            order[ch] = (moved[0:8] + moved[8:16]) + moved[16:24]
-        return 0
-
-    out[...] = jnp.zeros_like(out)
-    lax.fori_loop(0, LN // unroll, sort, 0)
-
-    def lay(ch, _):
-        src = (ch // 4) * 4 + (ch % 2) * 2 + (ch // 2) % 2
-        v = order[ch]
-        for d in range(4):
-            base = table[src, d]
-            start = table[src, 4 + d]
-            count = table[src, 8 + d]
-            w = base // LN
-            skip = base - w * LN
-            turned = pltpu.roll(v, lax.rem(skip - start + 2 * LN, LN), 1)
-            keep = (lane >= skip) & (lane < skip + count)
-            out[d, w] = jnp.where(keep, turned, out[d, w])
-            out[d, w + 1] = jnp.where(lane < skip + count - LN, turned, out[d, w + 1])
-        return 0
-
-    lax.fori_loop(0, LN, lay, 0, unroll=2)
-
-
-def exchange_kernel(subs, buf, out, local_sem, send_sem, recv_sem):
-    t, u = lax.axis_index("tile"), lax.axis_index("sub")
-    barrier = pltpu.get_barrier_semaphore()
-    for k in range(1, subs):
-        pl.semaphore_signal(barrier, inc=1, device_id=(t, lax.rem(u + k, subs)), device_id_type=MESH)
-    pl.semaphore_wait(barrier, subs - 1)
-    copies = []
-    for k in (2, 1, 3):
-        dst = lax.rem(u + k, subs)
-        copy = pltpu.make_async_remote_copy(
-            src_ref=buf.at[dst, pl.ds(0, TILES)],
-            dst_ref=out.at[pl.ds(u * TILES, TILES)],
-            send_sem=send_sem.at[k],
-            recv_sem=recv_sem.at[k],
-            device_id=(t, dst),
-            device_id_type=MESH,
-        )
-        copy.start()
-        copies.append(copy)
-    mine = pltpu.make_async_copy(buf.at[u, pl.ds(0, TILES)], out.at[pl.ds(u * TILES, TILES)], local_sem)
-    mine.start()
-    mine.wait()
-    for copy in copies:
-        copy.wait_send()
-    for copy in copies:
-        copy.wait_recv()
+    tiles[...] = jnp.zeros_like(tiles)
+
+    def lay(i, carry):
+        bases, currents = carry
+        new_bases, new_currents = [], []
+        at = (i & ~3) | ((i & 1) << 1) | ((i >> 1) & 1)
+        for src in range(subs):
+            base, current = bases[src], currents[src]
+            start, count = runs[src, at], runs[subs + src, at]
+            skip = base & (LN - 1)
+            end = skip + count
+            turned = pltpu.roll(gathered[src, at], (skip - start) & (LN - 1), 1)
+            merged = jnp.where(lane < skip, current, jnp.where(lane < end, turned, 0.0))
+            tiles[src, base >> 7] = merged
+            wrapped = jnp.where(lane < end - LN, turned, 0.0)
+            new_currents.append(jnp.where(end >= LN, wrapped, merged))
+            new_bases.append(base + count)
+        return tuple(new_bases), tuple(new_currents)
+
+    zero = jnp.zeros((8, LN), jnp.float32)
+    bases, currents = lax.fori_loop(
+        0, LN, lay, ((jnp.int32(0),) * subs, (zero,) * subs), unroll=2
+    )
+    for src in range(subs):
+        tiles[src, bases[src] >> 7] = currents[src]
+    for src in range(subs):
+        out[pl.ds(src * TILES, TILES)] = tiles[src, pl.ds(0, TILES)]
 
 
 def rows_of(a):
@@ -416,18 +488,14 @@
     tgt = rows_of(targets).reshape(LN, LN)
     vmem = pl.BlockSpec(memory_space=pltpu.VMEM)
     f32 = jnp.float32
-    pos, table = pl.pallas_call(
-        plan_kernel,
-        out_shape=[jax.ShapeDtypeStruct((LN, LN), jnp.int32)] * 2,
-        in_specs=[vmem],
+    gathered, runs = pl.pallas_call(
+        functools.partial(substeps_kernel, tiles, subs),
+        out_shape=[
+            jax.ShapeDtypeStruct((subs, LN, 8, LN), f32),
+            jax.ShapeDtypeStruct((2 * subs, LN), jnp.int32),
+        ],
+        in_specs=[vmem] * 6,
         out_specs=[vmem] * 2,
-        name="plan",
-    )(tgt)
-    state = pl.pallas_call(
-        functools.partial(substeps_kernel, tiles, subs),
-        out_shape=jax.ShapeDtypeStruct((8 * LN, LN), f32),
-        in_specs=[vmem] * 5,
-        out_specs=vmem,
         scratch_shapes=[
             pltpu.VMEM((4 * NF * 6, S, LN), f32),
             pltpu.VMEM((7, 2, 2, S, LN), f32),
@@ -441,29 +509,27 @@
             pltpu.VMEM((6, 3, 2, S, LN), f32),
             pltpu.VMEM((18 * 2 * S, 4, 8, LN), f32),
             pltpu.VMEM((18 * 2 * S, 4, 8, LN), f32),
+            pltpu.VMEM((4, 256, LN), f32),
+            pltpu.VMEM((LN, LN), jnp.int32),
+            pltpu.VMEM((subs, 2 * subs, LN), f32),
             pltpu.SemaphoreType.DMA((6, 8)),
             pltpu.SemaphoreType.DMA((6, 8)),
+            pltpu.SemaphoreType.DMA((4,)),
+            pltpu.SemaphoreType.DMA((4,)),
+            pltpu.SemaphoreType.DMA((3, 6)),
+            pltpu.SemaphoreType.DMA((3, 6)),
         ],
         compiler_params=pltpu.CompilerParams(collective_id=0, has_side_effects=True, vmem_limit_bytes=62 * 1024 * 1024),
         name="substeps",
-    )(off, vel, mas, ent, cnt)
-    buf = pl.pallas_call(
-        route_kernel,
-        out_shape=jax.ShapeDtypeStruct((subs, TILES + 2, 8, LN), f32),
-        in_specs=[pl.BlockSpec(memory_space=pltpu.SMEM), vmem, vmem],
+    )(off, vel, mas, ent, cnt, tgt)
+    arrived = pl.pallas_call(
+        lay_kernel,
+        out_shape=jax.ShapeDtypeStruct((subs * TILES, 8, LN), f32),
+        in_specs=[pl.BlockSpec(memory_space=pltpu.SMEM), vmem],
         out_specs=vmem,
-        scratch_shapes=[pltpu.VMEM((LN, 8, LN), f32)],
-        name="route",
-    )(table, pos, state)
-    arrived = pl.pallas_call(
-        functools.partial(exchange_kernel, subs),
-        out_shape=jax.ShapeDtypeStruct((subs * TILES, 8, LN), f32),
-        in_specs=[vmem],
-        out_specs=vmem,
-        scratch_shapes=[pltpu.SemaphoreType.DMA, pltpu.SemaphoreType.DMA((4,)), pltpu.SemaphoreType.DMA((4,))],
-        compiler_params=pltpu.CompilerParams(collective_id=1, has_side_effects=True),
-        name="exchange",
-    )(buf)
+        scratch_shapes=[pltpu.VMEM((subs, TILES + 2, 8, LN), f32)],
+        name="lay",
+    )(runs, gathered)
     return jnp.transpose(arrived, (1, 0, 2)).reshape(8, subs * TILES * LN)
 
 

time: 119 us -> 105 us (0.88)
  Pallas kernels: 116 us -> 105 us
  local copies, waits for them, and re-layouts: 2.06 us -> 0 us
    pallas_call x3 -> x1, Pallas kernels: 30.4 us -> 8.54 us  [shards(): pl.pallas_call(lay_kernel, out_shape=jax.ShapeDtypeStruct((subs * TILES,...]
    pallas_call x1, Pallas kernels: 85.8 us -> 96.1 us  [shards(): pl.pallas_call(functools.partial(substeps_kernel, tiles, subs), out_shape...]
    unnamed x1 -> x0, local copies, waits for them, and re-layouts: 2.06 us -> none
where the time goes in v3:
time: 105 us
  Pallas kernels  105 us (100%)
    pallas_call x1, Pallas kernels, shards(): pl.pallas_call(functools.partial(substeps_kernel, tiles, subs), out_shape...  96.1 us
    pallas_call x1, Pallas kernels, shards(): pl.pallas_call(lay_kernel, out_shape=jax.ShapeDtypeStruct((subs * TILES,...  8.54 us

profile of v3, /device:TPU:0, one launch (start us, length us, event | category | flops | bytes accessed | tf_op | source)
XLA Modules:
  0.0 104.7 jit_solution(4416983478177508915)
XLA Ops:
  0.0 96.1 %substeps.1 = (f32[4,128,8,128]{3,2,1,0:T(8,128)}, s32[8,128]{1,0:T(8,128)}) custom-call(f32[3,128,128]{2,1,0:T(8,128)} %bitcast.33, f32[3,128,128]{2,1,0:T(8,128)} %bitcast.34, f32[128,128]{1,0:T(8,128)} %bitcast.35, f32[128,128]{1,0:T(8,128)} %bitcast.36, s32[3,4,128]{2,1,0:T(4,128)} %bitcast.38, s32[128,128]{1,0:T(8,128)} %bitcast.37), custom_call_target="tpu_custom_call" | custom-call | tf_op jit(solution)/shard_map/substeps/pallas_call | solution.py:491
  96.1 8.5 %lay.1 = f32[192,8,128]{2,1,0:T(8,128)} custom-call(s32[8,128]{1,0:T(8,128)} %get-tuple-element.7.runs, f32[4,128,8,128]{3,2,1,0:T(8,128)} %get-tuple-element.8.gathered), custom_call_target="tpu_custom_call" | custom-call | tf_op jit(solution)/shard_map/lay/pallas_call | solution.py:525

commit v4 on v3

--- a/solution.py
+++ b/solution.py
@@ -93,8 +93,8 @@
                 pltpu.make_async_remote_copy(
                     src_ref=src.at[pl.ds(0, ncomp), row, :, pl.ds(0, n)],
                     dst_ref=inbox.at[rnd // 2, slot, pl.ds(0, ncomp), :, pl.ds(0, n)],
-                    send_sem=send_sem.at[rnd, f],
-                    recv_sem=recv_sem.at[rnd, f],
+                    send_sem=send_sem.at[rnd % 2, f],
+                    recv_sem=recv_sem.at[rnd % 2, f],
                     device_id=(dst_t, u),
                     device_id_type=MESH,
                 )
@@ -106,8 +106,8 @@
                     pltpu.make_async_remote_copy(
                         src_ref=ysend.at[rnd, side, pl.ds(0, n)],
                         dst_ref=yin.at[rnd, 2 - dt, 1 - side, pl.ds(0, n)],
-                        send_sem=send_sem.at[rnd, f],
-                        recv_sem=recv_sem.at[rnd, f],
+                        send_sem=send_sem.at[rnd % 2, f],
+                        recv_sem=recv_sem.at[rnd % 2, f],
                         device_id=(tile_of[dt], right if side == 1 else left),
                         device_id_type=MESH,
                     )
@@ -156,7 +156,7 @@
     def own(row, comp, h, g, n):
         return fld[field(row + 1, comp, 1, h), pl.ds(g * 8, n * 8), :].reshape(n, 8, LN)
 
-    def density_stage(stage, k):
+    def density_stage(stage, k, first=0, last=2):
         per = NACT[k] // 8
         halves = 2 if per == 1 else 1
         base = STAGE_BASE[stage]
@@ -187,9 +187,10 @@
                 pairs(i // 2, i % 2)
             return 0
 
-        lax.fori_loop(0, STAGE_SIZE[stage] * 2 // halves, combo, 0)
-
-    def force_stage(stage, k):
+        per_row = STAGE_SIZE[stage] // halves
+        lax.fori_loop(first * per_row, last * per_row, combo, 0)
+
+    def force_stage(stage, k, first=0, last=2):
         groups = NACT[k] // 8
         per = min(groups, 2)
         sets = groups // per
@@ -229,7 +230,8 @@
                 pairs(ch // 2, ch % 2, g)
             return 0
 
-        lax.fori_loop(0, STAGE_SIZE[stage] * 2 * sets // halves, combo, 0)
+        per_row = STAGE_SIZE[stage] * sets // halves
+        lax.fori_loop(first * per_row, last * per_row, combo, 0)
 
     def plan():
         row_i = lax.broadcasted_iota(jnp.int32, (LN, LN), 0)
@@ -270,9 +272,9 @@
             sends.append(copy)
         return sends
 
-    def emit(g):
+    def emit(g, own_rows):
         row_q = lax.broadcasted_iota(jnp.int32, (LN, LN), 0)
-        for row in range(2):
+        for row in own_rows:
             for h in range(2):
                 count = jnp.broadcast_to(cnt[0, pl.ds(h * 2 + row, 1), :], (8, LN))
                 rows = pl.ds(g * 8, 8)
@@ -283,13 +285,15 @@
                 values += [pr[2, row, h, rows, :] * 0.25]
                 values += [jnp.where(slot < count, mass[in_rows, :], 0.0)]
                 for i, v in enumerate(values):
-                    raw[g, pl.ds((h * 2 + row) * 64 + i, 8, stride=8), :] = v
-
-        def sort(hr, _):
+                    raw[g, pl.ds((row * 2 + h) * 64 + i, 8, stride=8), :] = v
+
+        def sort(rh, _):
+            row, h = rh // 2, rh % 2
             for i in range(8):
-                at = (g * 8 + i) * 4 + hr
-                hot = jnp.where(row_q == jnp.broadcast_to(pos[pl.ds(at, 1), :], (LN, LN)), 1.0, 0.0)
-                v = raw[g, pl.ds(hr * 64 + i * 8, 8), :]
+                slot = g * 8 + i
+                line = pos[pl.ds(slot * 4 + h * 2 + row, 1), :]
+                hot = jnp.where(row_q == jnp.broadcast_to(line, (LN, LN)), 1.0, 0.0)
+                v = raw[g, pl.ds(rh * 64 + i * 8, 8), :]
                 hi = v.astype(jnp.bfloat16)
                 rest = v - hi.astype(jnp.float32)
                 mid = rest.astype(jnp.bfloat16)
@@ -298,17 +302,21 @@
                 moved = lax.dot_general(
                     pieces, hot.astype(jnp.bfloat16), (((1,), (1,)), ((), ())), preferred_element_type=jnp.float32
                 )
-                gathered[u, at] = (moved[0:8] + moved[8:16]) + moved[16:24]
+                gathered[u, slot * 2 + h, row] = (moved[0:8] + moved[8:16]) + moved[16:24]
             return 0
 
-        lax.fori_loop(0, 4, sort, 0)
-
-    PIECES = ((64, 64), (32, 32), (0, 32))
-
-    def piece_copy(p, flow, owner, first, rows, dst):
+        lax.fori_loop(own_rows[0] * 2, own_rows[-1] * 2 + 2, sort, 0)
+
+    PIECES = ((32, 32, (0, 1)), (16, 16, (0, 1)), (0, 16, (0,)), (0, 16, (1,)))
+
+    def piece_copy(p, flow, owner, second_half, dst):
+        first, rows, own_rows = PIECES[p]
+        half = rows // 2
+        part = pl.ds(first + half * second_half, half)
+        which = slice(None) if len(own_rows) == 2 else own_rows[0]
         return pltpu.make_async_remote_copy(
-            src_ref=gathered.at[owner, pl.ds(first, rows)],
-            dst_ref=gathered.at[owner, pl.ds(first, rows)],
+            src_ref=gathered.at[owner, part, which],
+            dst_ref=gathered.at[owner, part, which],
             send_sem=piece_send.at[p, flow],
             recv_sem=piece_recv.at[p, flow],
             device_id=(t, dst),
@@ -316,32 +324,34 @@
         )
 
     def start_piece(p):
-        first, rows = PIECES[p]
-        for g in range(first // 32, (first + rows) // 32):
-            emit(g)
-        half = rows // 2
+        first, rows, own_rows = PIECES[p]
+        for g in range(first // 16, (first + rows) // 16):
+            emit(g, own_rows)
         copies = [
-            piece_copy(p, 0, u, first, half, right),
-            piece_copy(p, 1, u, first + half, half, right),
-            piece_copy(p, 2, u, first + half, half, left),
-            piece_copy(p, 3, u, first, half, left),
+            piece_copy(p, 0, u, 0, right),
+            piece_copy(p, 1, u, 1, right),
+            piece_copy(p, 2, u, 1, left),
+            piece_copy(p, 3, u, 0, left),
         ]
         for f in (0, 2, 1, 3):
             copies[f].start()
-        return copies
+        arriving[p] = copies
 
     def forward_piece(p):
-        first, rows = PIECES[p]
-        half = rows // 2
-        copies = [
-            piece_copy(p, 4, left, first, half, right),
-            piece_copy(p, 5, right, first + half, half, left),
-        ]
+        arriving[p][0].wait_recv()
+        arriving[p][2].wait_recv()
+        copies = [piece_copy(p, 4, left, 0, right), piece_copy(p, 5, right, 1, left)]
         for copy in copies:
             copy.start()
-        return copies
-
-    def exchange_and_sum(rnd, src, inbox, comps, n, stage_fn, k, meanwhile):
+        arriving[p] += copies
+
+    def finish_piece(p):
+        for f in (1, 3, 4, 5):
+            arriving[p][f].wait_recv()
+        for copy in arriving[p]:
+            copy.wait_send()
+
+    def exchange_and_sum(rnd, src, inbox, comps, n, stage_fn, k, meanwhile, row_done=None):
         copies = start_round(rnd, src, len(comps), n, inbox)
         meanwhile()
         loads = [None] * 4
@@ -356,29 +366,82 @@
         copies[5].wait_recv()
         for r in (1, 2):
             sides(loads[r], comps, r, n, rnd, 1, r - 1)
-        stage_fn(1, k)
+        stage_fn(1, k, 0, 2 if row_done is None else 1)
         for f in (0, 1, 2, 3, 6, 7):
             copies[f].wait_recv()
         for r, dt, sender_row in ((0, 0, 1), (3, 2, 0)):
             centre(loads[r], comps, r, n)
             sides(loads[r], comps, r, n, rnd, dt, sender_row)
-        stage_fn(2, k)
-        return copies
-
-    pending = []
+        if row_done is None:
+            stage_fn(2, k)
+            return copies
+        for copy in copies:
+            copy.wait_send()
+        stage_fn(2, k, 0, 1)
+        row_done(0)
+        stage_fn(1, k, 1, 2)
+        row_done(1)
+        stage_fn(2, k, 1, 2)
+        row_done(2)
+        return []
+
     arriving = {}
+
+    def lay_plan():
+        for copy in arriving["tab"]:
+            copy.wait_recv()
+        row_i = lax.broadcasted_iota(jnp.int32, (LN, LN), 0)
+        col_i = lax.broadcasted_iota(jnp.int32, (LN, LN), 1)
+
+        def order(i):
+            return (i // 4) * 4 + (i % 2) * 2 + (i // 2) % 2
+
+        earlier = jnp.where(order(row_i) < order(col_i), 1.0, 0.0).astype(jnp.bfloat16)
+        starts = jnp.concatenate([tab[src, pl.ds(u, 1), :] for src in range(subs)], axis=0)
+        counts = jnp.concatenate([tab[src, pl.ds(subs + u, 1), :] for src in range(subs)], axis=0)
+        padded = jnp.concatenate([counts, jnp.zeros_like(counts)], axis=0).astype(jnp.bfloat16)
+        base = jnp.dot(padded, earlier, preferred_element_type=jnp.float32)[0:subs]
+        base = base.astype(jnp.int32)
+        skip = base & (LN - 1)
+        runs[0:subs, :] = (skip - starts.astype(jnp.int32)) & (LN - 1)
+        runs[subs : 2 * subs, :] = skip
+        runs[2 * subs : 3 * subs, :] = skip + counts.astype(jnp.int32)
+        runs[3 * subs : 4 * subs, :] = base >> 7
 
     def during(rnd):
         if rnd == 0:
             arriving["tab"] = plan()
+        elif rnd == 1:
+            lay_plan()
         elif rnd in (2, 4):
-            arriving[rnd] = start_piece(rnd // 2 - 1)
+            start_piece(rnd // 2 - 1)
         elif rnd in (3, 5):
-            p = rnd // 2 - 1
-            copies = arriving[rnd - 1]
-            copies[0].wait_recv()
-            copies[2].wait_recv()
-            arriving[rnd] = forward_piece(p)
+            forward_piece(rnd // 2 - 1)
+
+    def move(k, row):
+        for h in range(2):
+            count = jnp.broadcast_to(cnt[k, pl.ds(h * 2 + row, 1), :], (8, LN))
+            for g in range(NACT[k] // 8):
+                rows = pl.ds(g * 8, 8)
+                slot = lax.broadcasted_iota(jnp.int32, (8, LN), 0) + g * 8
+                active = slot < count
+                for d in range(3):
+                    v = st[3 + d, row, h, rows, :]
+                    x = st[d, row, h, rows, :]
+                    v_new = v + 4.0 * acc[d, row, h, rows, :]
+                    st[3 + d, row, h, rows, :] = jnp.where(active, v_new, v)
+                    st[d, row, h, rows, :] = jnp.where(active, x + 0.0125 * v_new, x)
+
+    def last_rows(step):
+        if step == 0:
+            move(2, 0)
+            start_piece(2)
+        elif step == 1:
+            forward_piece(2)
+        else:
+            move(2, 1)
+            start_piece(3)
+            forward_piece(3)
 
     for k in range(3):
         n = NACT[k]
@@ -397,44 +460,21 @@
                     pr[1, row, h, rows, :] = sq[1, row, h, rows, :] * root
                     pr[2, row, h, rows, :] = rho4
         acc[...] = jnp.zeros_like(acc)
-        pressed = exchange_and_sum(2 * k + 1, pr, pin, (Q, C, R), n, force_stage, k, lambda: during(2 * k + 1))
-        for copy in moved + pressed:
-            copy.wait_send()
-        for row in range(2):
-            for h in range(2):
-                count = jnp.broadcast_to(cnt[k, pl.ds(h * 2 + row, 1), :], (8, LN))
-                for g in range(n // 8):
-                    rows = pl.ds(g * 8, 8)
-                    slot = lax.broadcasted_iota(jnp.int32, (8, LN), 0) + g * 8
-                    active = slot < count
-                    for d in range(3):
-                        v = st[3 + d, row, h, rows, :]
-                        x = st[d, row, h, rows, :]
-                        v_new = v + 4.0 * acc[d, row, h, rows, :]
-                        st[3 + d, row, h, rows, :] = jnp.where(active, v_new, v)
-                        st[d, row, h, rows, :] = jnp.where(active, x + 0.0125 * v_new, x)
-    for rnd in (3, 5):
-        direct, passed = arriving[rnd - 1], arriving[rnd]
-        pending += direct + passed
-        for copy in (direct[1], direct[3], passed[0], passed[1]):
-            copy.wait_recv()
-    pending += arriving["tab"]
+        if k == 2:
+            for copy in moved:
+                copy.wait_send()
+        pressed = exchange_and_sum(
+            2 * k + 1, pr, pin, (Q, C, R), n, force_stage, k, lambda: during(2 * k + 1), last_rows if k == 2 else None
+        )
+        if k < 2:
+            for copy in moved + pressed:
+                copy.wait_send()
+            for row in range(2):
+                move(k, row)
     for copy in arriving["tab"]:
-        copy.wait_recv()
-
-
-    copies = start_piece(2)
-    copies[0].wait_recv()
-    copies[2].wait_recv()
-    forward = forward_piece(2)
-    pending += copies + forward
-    for src in range(subs):
-        runs[src : src + 1, :] = tab[src, pl.ds(u, 1), :].astype(jnp.int32)
-        runs[subs + src : subs + src + 1, :] = tab[src, pl.ds(subs + u, 1), :].astype(jnp.int32)
-    for copy in pending:
         copy.wait_send()
-    for copy in (copies[1], copies[3], forward[0], forward[1]):
-        copy.wait_recv()
+    for p in range(4):
+        finish_piece(p)
 
 
 TILES = 48
@@ -443,31 +483,30 @@
 def lay_kernel(runs, gathered, out, tiles):
     subs = gathered.shape[0]
     lane = lane_iota()
+    beyond = lane + LN
     tiles[...] = jnp.zeros_like(tiles)
 
-    def lay(i, carry):
-        bases, currents = carry
-        new_bases, new_currents = [], []
-        at = (i & ~3) | ((i & 1) << 1) | ((i >> 1) & 1)
-        for src in range(subs):
-            base, current = bases[src], currents[src]
-            start, count = runs[src, at], runs[subs + src, at]
-            skip = base & (LN - 1)
-            end = skip + count
-            turned = pltpu.roll(gathered[src, at], (skip - start) & (LN - 1), 1)
-            merged = jnp.where(lane < skip, current, jnp.where(lane < end, turned, 0.0))
-            tiles[src, base >> 7] = merged
-            wrapped = jnp.where(lane < end - LN, turned, 0.0)
-            new_currents.append(jnp.where(end >= LN, wrapped, merged))
-            new_bases.append(base + count)
-        return tuple(new_bases), tuple(new_currents)
+    def lay(slot, currents):
+        for row in range(2):
+            for h in range(2):
+                at = slot * 4 + h * 2 + row
+                later = []
+                for src in range(subs):
+                    end = jnp.full((8, LN), runs[2 * subs + src, at])
+                    turned = pltpu.roll(gathered[src, slot * 2 + h, row], runs[src, at], 1)
+                    kept = jnp.where(lane < end, turned, 0.0)
+                    merged = jnp.where(lane < runs[subs + src, at], currents[src], kept)
+                    tiles[src, runs[3 * subs + src, at]] = merged
+                    wrapped = jnp.where(beyond < end, turned, 0.0)
+                    later.append(jnp.where(end >= LN, wrapped, merged))
+                currents = later
+        return tuple(currents)
 
     zero = jnp.zeros((8, LN), jnp.float32)
-    bases, currents = lax.fori_loop(
-        0, LN, lay, ((jnp.int32(0),) * subs, (zero,) * subs), unroll=2
-    )
+    currents = lax.fori_loop(0, S, lay, (zero,) * subs)
     for src in range(subs):
-        tiles[src, bases[src] >> 7] = currents[src]
+        last = runs[2 * subs + src, LN - 1]
+        tiles[src, runs[3 * subs + src, LN - 1] + jnp.where(last >= LN, 1, 0)] = currents[src]
     for src in range(subs):
         out[pl.ds(src * TILES, TILES)] = tiles[src, pl.ds(0, TILES)]
 
@@ -491,8 +530,8 @@
     gathered, runs = pl.pallas_call(
         functools.partial(substeps_kernel, tiles, subs),
         out_shape=[
-            jax.ShapeDtypeStruct((subs, LN, 8, LN), f32),
-            jax.ShapeDtypeStruct((2 * subs, LN), jnp.int32),
+            jax.ShapeDtypeStruct((subs, LN // 2, 2, 8, LN), f32),
+            jax.ShapeDtypeStruct((4 * subs, LN), jnp.int32),
         ],
         in_specs=[vmem] * 6,
         out_specs=[vmem] * 2,
@@ -512,12 +551,12 @@
             pltpu.VMEM((4, 256, LN), f32),
             pltpu.VMEM((LN, LN), jnp.int32),
             pltpu.VMEM((subs, 2 * subs, LN), f32),
-            pltpu.SemaphoreType.DMA((6, 8)),
-            pltpu.SemaphoreType.DMA((6, 8)),
+            pltpu.SemaphoreType.DMA((2, 8)),
+            pltpu.SemaphoreType.DMA((2, 8)),
             pltpu.SemaphoreType.DMA((4,)),
             pltpu.SemaphoreType.DMA((4,)),
-            pltpu.SemaphoreType.DMA((3, 6)),
-            pltpu.SemaphoreType.DMA((3, 6)),
+            pltpu.SemaphoreType.DMA((4, 6)),
+            pltpu.SemaphoreType.DMA((4, 6)),
         ],
         compiler_params=pltpu.CompilerParams(collective_id=0, has_side_effects=True, vmem_limit_bytes=62 * 1024 * 1024),
         name="substeps",

time: 105 us -> 104 us (level)
    pallas_call x1, Pallas kernels: 8.54 us -> 5.46 us  [shards(): pl.pallas_call(lay_kernel, out_shape=jax.ShapeDtypeStruct((subs * TILES,...]
    pallas_call x1, Pallas kernels: 96.1 us -> 98.2 us  [shards(): pl.pallas_call(functools.partial(substeps_kernel, tiles, subs), out_shape...]
where the time goes in v4:
time: 104 us
  Pallas kernels  104 us (100%)
    pallas_call x1, Pallas kernels, shards(): pl.pallas_call(functools.partial(substeps_kernel, tiles, subs), out_shape...  98.2 us
    pallas_call x1, Pallas kernels, shards(): pl.pallas_call(lay_kernel, out_shape=jax.ShapeDtypeStruct((subs * TILES,...  5.46 us

profile of v4, /device:TPU:0, one launch (start us, length us, event | category | flops | bytes accessed | tf_op | source)
XLA Modules:
  0.0 103.7 jit_solution(3517386634897550559)
XLA Ops:
  0.0 98.2 %substeps.1 = (f32[4,64,2,8,128]{4,3,2,1,0:T(8,128)}, s32[16,128]{1,0:T(8,128)}) custom-call(f32[3,128,128]{2,1,0:T(8,128)} %bitcast.33, f32[3,128,128]{2,1,0:T(8,128)} %bitcast.34, f32[128,128]{1,0:T(8,128)} %bitcast.35, f32[128,128]{1,0:T(8,128)} %bitcast.36, s32[3,4,128]{2,1,0:T(4,128)} %bitcast.38, s32[128,128]{1,0:T(8,128)} %bitcast.37), custom_call_target="tpu_custom_call" | custom-call | tf_op jit(solution)/shard_map/substeps/pallas_call | solution.py:530
  98.2 5.5 %lay.1 = f32[192,8,128]{2,1,0:T(8,128)} custom-call(s32[16,128]{1,0:T(8,128)} %get-tuple-element.7.runs, f32[4,64,2,8,128]{4,3,2,1,0:T(8,128)} %get-tuple-element.8.gathered), custom_call_target="tpu_custom_call" | custom-call | tf_op jit(solution)/shard_map/lay/pallas_call | solution.py:564

commit v5 on v4

--- a/solution.py
+++ b/solution.py
@@ -41,8 +41,8 @@
 
 
 def substeps_kernel(
-    tiles, subs, off, vel, mass, ent, cnt, tgt, gathered, runs, fld, st, pr, dens, acc, sq, ysend, xin, pin, yin,
-    cache_w, cache_a, raw, pos, tab, send_sem, recv_sem, tab_send, tab_recv, piece_send, piece_recv
+    tiles, subs, off, vel, mass, ent, cnt, tgt, done, runs, gathered, fld, st, pr, dens, acc, sq, ysend, xin, pin, yin,
+    cache_w, cache_a, raw, pos, tab, send_sem, recv_sem, tab_send, tab_recv, piece_send, piece_recv, done_sem
 ):
     t, u = lax.axis_index("tile"), lax.axis_index("sub")
     up, down = lax.rem(t + 1, tiles), lax.rem(t + tiles - 1, tiles)
@@ -323,7 +323,7 @@
             device_id_type=MESH,
         )
 
-    def start_piece(p):
+    def start_piece(p, before_rest=None):
         first, rows, own_rows = PIECES[p]
         for g in range(first // 16, (first + rows) // 16):
             emit(g, own_rows)
@@ -333,9 +333,13 @@
             piece_copy(p, 2, u, 1, left),
             piece_copy(p, 3, u, 0, left),
         ]
-        for f in (0, 2, 1, 3):
-            copies[f].start()
         arriving[p] = copies
+        copies[0].start()
+        copies[2].start()
+        if before_rest is not None:
+            before_rest()
+        copies[1].start()
+        copies[3].start()
 
     def forward_piece(p):
         arriving[p][0].wait_recv()
@@ -345,11 +349,20 @@
             copy.start()
         arriving[p] += copies
 
+    leaving = []
+
     def finish_piece(p):
         for f in (1, 3, 4, 5):
             arriving[p][f].wait_recv()
         for copy in arriving[p]:
             copy.wait_send()
+        first, rows, own_rows = PIECES[p]
+        which = slice(None) if len(own_rows) == 2 else own_rows[0]
+        copy = pltpu.make_async_copy(
+            gathered.at[:, pl.ds(first, rows), which], done.at[:, pl.ds(first, rows), which], done_sem.at[p]
+        )
+        copy.start()
+        leaving.append(copy)
 
     def exchange_and_sum(rnd, src, inbox, comps, n, stage_fn, k, meanwhile, row_done=None):
         copies = start_round(rnd, src, len(comps), n, inbox)
@@ -414,6 +427,8 @@
         elif rnd == 1:
             lay_plan()
         elif rnd in (2, 4):
+            if rnd == 4:
+                finish_piece(0)
             start_piece(rnd // 2 - 1)
         elif rnd in (3, 5):
             forward_piece(rnd // 2 - 1)
@@ -436,11 +451,10 @@
         if step == 0:
             move(2, 0)
             start_piece(2)
-        elif step == 1:
-            forward_piece(2)
-        else:
+        elif step == 2:
+            finish_piece(1)
             move(2, 1)
-            start_piece(3)
+            start_piece(3, lambda: forward_piece(2))
             forward_piece(3)
 
     for k in range(3):
@@ -473,23 +487,33 @@
                 move(k, row)
     for copy in arriving["tab"]:
         copy.wait_send()
-    for p in range(4):
+    for p in (2, 3):
         finish_piece(p)
+    for copy in leaving:
+        copy.wait()
 
 
 TILES = 48
 
 
-def lay_kernel(runs, gathered, out, tiles):
+STEPS = 4
+
+
+def lay_kernel(runs, gathered, out, tiles, edge):
     subs = gathered.shape[0]
     lane = lane_iota()
     beyond = lane + LN
-    tiles[...] = jnp.zeros_like(tiles)
+    step = pl.program_id(0)
+
+    @pl.when(step == 0)
+    def _():
+        tiles[...] = jnp.zeros_like(tiles)
+        edge[...] = jnp.zeros_like(edge)
 
     def lay(slot, currents):
         for row in range(2):
             for h in range(2):
-                at = slot * 4 + h * 2 + row
+                at = (step * (S // STEPS) + slot) * 4 + h * 2 + row
                 later = []
                 for src in range(subs):
                     end = jnp.full((8, LN), runs[2 * subs + src, at])
@@ -502,13 +526,17 @@
                 currents = later
         return tuple(currents)
 
-    zero = jnp.zeros((8, LN), jnp.float32)
-    currents = lax.fori_loop(0, S, lay, (zero,) * subs)
+    currents = lax.fori_loop(0, S // STEPS, lay, tuple(edge[src] for src in range(subs)))
     for src in range(subs):
-        last = runs[2 * subs + src, LN - 1]
-        tiles[src, runs[3 * subs + src, LN - 1] + jnp.where(last >= LN, 1, 0)] = currents[src]
-    for src in range(subs):
-        out[pl.ds(src * TILES, TILES)] = tiles[src, pl.ds(0, TILES)]
+        edge[src] = currents[src]
+
+    @pl.when(step == STEPS - 1)
+    def _():
+        for src in range(subs):
+            last = runs[2 * subs + src, LN - 1]
+            tiles[src, runs[3 * subs + src, LN - 1] + jnp.where(last >= LN, 1, 0)] = currents[src]
+        for src in range(subs):
+            out[pl.ds(src * TILES, TILES)] = tiles[src, pl.ds(0, TILES)]
 
 
 def rows_of(a):
@@ -534,8 +562,9 @@
             jax.ShapeDtypeStruct((4 * subs, LN), jnp.int32),
         ],
         in_specs=[vmem] * 6,
-        out_specs=[vmem] * 2,
+        out_specs=[pl.BlockSpec(memory_space=pl.ANY), vmem],
         scratch_shapes=[
+            pltpu.VMEM((subs, LN // 2, 2, 8, LN), f32),
             pltpu.VMEM((4 * NF * 6, S, LN), f32),
             pltpu.VMEM((7, 2, 2, S, LN), f32),
             pltpu.VMEM((3, 2, 2, S, LN), f32),
@@ -557,16 +586,21 @@
             pltpu.SemaphoreType.DMA((4,)),
             pltpu.SemaphoreType.DMA((4, 6)),
             pltpu.SemaphoreType.DMA((4, 6)),
+            pltpu.SemaphoreType.DMA((4,)),
         ],
         compiler_params=pltpu.CompilerParams(collective_id=0, has_side_effects=True, vmem_limit_bytes=62 * 1024 * 1024),
         name="substeps",
     )(off, vel, mas, ent, cnt, tgt)
     arrived = pl.pallas_call(
         lay_kernel,
+        grid=(STEPS,),
         out_shape=jax.ShapeDtypeStruct((subs * TILES, 8, LN), f32),
-        in_specs=[pl.BlockSpec(memory_space=pltpu.SMEM), vmem],
-        out_specs=vmem,
-        scratch_shapes=[pltpu.VMEM((subs, TILES + 2, 8, LN), f32)],
+        in_specs=[
+            pl.BlockSpec(memory_space=pltpu.SMEM),
+            pl.BlockSpec((subs, LN // 2 // STEPS, 2, 8, LN), lambda i: (0, i, 0, 0, 0)),
+        ],
+        out_specs=pl.BlockSpec((subs * TILES, 8, LN), lambda i: (0, 0, 0)),
+        scratch_shapes=[pltpu.VMEM((subs, TILES + 2, 8, LN), f32), pltpu.VMEM((subs, 8, LN), f32)],
         name="lay",
     )(runs, gathered)
     return jnp.transpose(arrived, (1, 0, 2)).reshape(8, subs * TILES * LN)

time: 104 us -> 101 us (0.971)
  Pallas kernels: 104 us -> 101 us
    pallas_call x1, Pallas kernels: 98.2 us -> 95.6 us  [shards(): pl.pallas_call(functools.partial(substeps_kernel, tiles, subs), out_shape...]
where the time goes in v5:
time: 101 us
  Pallas kernels  101 us (100%)
    pallas_call x1, Pallas kernels, shards(): pl.pallas_call(functools.partial(substeps_kernel, tiles, subs), out_shape...  95.6 us
    pallas_call x1, Pallas kernels, shards(): pl.pallas_call(lay_kernel, grid=(STEPS,), out_shape=jax.ShapeDtypeStruct(...  5.54 us

profile of v5, /device:TPU:0, one launch (start us, length us, event | category | flops | bytes accessed | tf_op | source)
XLA Modules:
  0.0 101.1 jit_solution(10560594113005775995)
XLA Ops:
  0.0 95.6 %substeps.1 = (f32[4,64,2,8,128]{4,3,2,1,0:T(8,128)}, s32[16,128]{1,0:T(8,128)}) custom-call(f32[3,128,128]{2,1,0:T(8,128)} %bitcast.33, f32[3,128,128]{2,1,0:T(8,128)} %bitcast.34, f32[128,128]{1,0:T(8,128)} %bitcast.35, f32[128,128]{1,0:T(8,128)} %bitcast.36, s32[3,4,128]{2,1,0:T(4,128)} %bitcast.38, s32[128,128]{1,0:T(8,128)} %bitcast.37), custom_call_target="tpu_custom_call" | custom-call | tf_op jit(solution)/shard_map/substeps/pallas_call | solution.py:558
  95.6 5.5 %lay.1 = f32[192,8,128]{2,1,0:T(8,128)} custom-call(s32[16,128]{1,0:T(8,128)} %get-tuple-element.7.runs, f32[4,64,2,8,128]{4,3,2,1,0:T(8,128)} %get-tuple-element.8.gathered), custom_call_target="tpu_custom_call" | custom-call | tf_op jit(solution)/shard_map/lay/pallas_call | solution.py:594

commit v6 on v5

--- a/solution.py
+++ b/solution.py
@@ -42,7 +42,7 @@
 
 def substeps_kernel(
     tiles, subs, off, vel, mass, ent, cnt, tgt, done, runs, gathered, fld, st, pr, dens, acc, sq, ysend, xin, pin, yin,
-    cache_w, cache_a, raw, pos, tab, send_sem, recv_sem, tab_send, tab_recv, piece_send, piece_recv, done_sem
+    cache_w, cache_a, raw, back, pos, tab, send_sem, recv_sem, tab_send, tab_recv, piece_send, piece_recv, done_sem
 ):
     t, u = lax.axis_index("tile"), lax.axis_index("sub")
     up, down = lax.rem(t + 1, tiles), lax.rem(t + tiles - 1, tiles)
@@ -156,16 +156,151 @@
     def own(row, comp, h, g, n):
         return fld[field(row + 1, comp, 1, h), pl.ds(g * 8, n * 8), :].reshape(n, 8, LN)
 
+    EDGE_SLOT = 14
+
+    def edges(comps):
+        for comp in comps:
+            for g in range(4):
+                rows = pl.ds(g * 8, 8)
+
+                def packed(zero, one, two, three):
+                    v = fld[zero, rows, :]
+                    v = jnp.where(lane == 1, pltpu.roll(fld[one, rows, :], 1, 1), v)
+                    v = jnp.where(lane == 2, pltpu.roll(fld[two, rows, :], 2, 1), v)
+                    return jnp.where(lane == 3, pltpu.roll(fld[three, rows, :], 4, 1), v)
+
+                low0, low1 = field(1, comp, 1, 0), field(2, comp, 1, 0)
+                fld[field(4, comp, 1, 0), rows, :] = packed(low0, low1, low1, field(2, comp, 1, 1))
+                low0, low1 = field(1, comp, 0, 0), field(2, comp, 0, 0)
+                fld[field(4, comp, 0, 0), rows, :] = packed(low0, low1, low0, field(1, comp, 2, 1))
+
+    def spread_edges(sums):
+        for g in range(4):
+            rows = pl.ds(g * 8, 8)
+            v = sums[2, 1, rows, :]
+            one_two = pltpu.roll(v, 127, 1) + pltpu.roll(v, 126, 1)
+            sums[0, 1, rows, :] += jnp.where(lane == 0, v, 0.0)
+            sums[1, 1, rows, :] += jnp.where(lane == 0, one_two, 0.0)
+            sums[1, 2, rows, :] += jnp.where(lane == 127, pltpu.roll(v, 124, 1), 0.0)
+
+    def paired_stage(stage, body):
+        if stage == 0:
+
+            def alone(i, _):
+                body(i // 2, 1 + i // 2, 1, i % 2, i, True)
+                return 0
+
+            def straight(h, _):
+                body(0, 2, 1, h, 4 + h, False)
+                return 0
+
+            lax.fori_loop(0, 4, alone, 0)
+            lax.fori_loop(0, 2, straight, 0)
+        else:
+
+            def slanted(ih, _):
+                i, h = ih // 2, ih % 2
+                body(i // 3, 1 + (i + 2) // 3, 2 - 2 * (i // 2 - i // 3), h, 6 + ih, False, True)
+                return 0
+
+            lax.fori_loop(0, 8, slanted, 0)
+
+    def give_back(sums, which, r, b, h, alone, shifted, sign):
+        for jg in range(2 if alone else 0, 4):
+            rows = pl.ds(jg * 8, 8)
+            part = back[which, pl.ds(jg * 64, 8, stride=8), :]
+            for sub in range(1, 8):
+                part = part + back[which, pl.ds(jg * 64 + sub, 8, stride=8), :]
+            part = part * sign if sign != 1.0 else part
+            if not shifted:
+                sums[r - 1, 1 + h, rows, :] += part
+            else:
+                part = pltpu.roll(part, (b + (LN - 1)) % LN, 1)
+                over = lane == (LN - 1) * (1 - b // 2)
+                sums[r - 1, 1 + h, rows, :] += jnp.where(over, 0.0, part)
+                sums[r - 1, h + b, rows, :] += jnp.where(over, part, 0.0)
+
+    def density_paired(row, r, b, h, slot, alone, shifted=False):
+        mine = [[own(row, comp, h, g, 2) for comp in (X, Y, Z, MS)] for g in (0, 2)]
+        totals = [dens[row, 1 + h, pl.ds(g * 8, 16), :].reshape(2, 8, LN) for g in (0, 2)]
+        for j in range(S):
+            given = None
+            mj = other(r, MS, b, h, j)
+            for g in (0,) if alone and j < 16 else (0, 1):
+                xi, yi, zi, mi = mine[g]
+                dx = xi - other(r, X, b, h, j)
+                dy = yi - other(r, Y, b, h, j)
+                dz = zi - other(r, Z, b, h, j)
+                r2 = dx * dx + dy * dy + dz * dz
+                rad = r2 * lax.rsqrt(jnp.maximum(r2, 1e-30))
+                s = jnp.maximum(4.0 - rad, 0.0)
+                s3 = s * (s * s)
+                w = s3 * (s * (5.0 - s))
+                totals[g] = totals[g] + w * mj
+                cache_w[slot * S + j, pl.ds(g * 2, 2)] = s3
+                cache_a[slot * S + j, pl.ds(g * 2, 2)] = 1.0 / (r2 + 0.16)
+                if not alone or (g == 0 and j >= 16):
+                    wi = w * mi
+                    wi = wi[0] + wi[1]
+                    given = wi if given is None else given + wi
+            if given is not None:
+                back[0, pl.ds(j * 8, 8), :] = given
+        for g in (0, 1):
+            dens[row, 1 + h, pl.ds(g * 16, 16), :] = totals[g].reshape(16, LN)
+        give_back(dens, 0, r, b, h, alone, shifted, 1.0)
+
+    def force_paired(row, r, b, h, slot, alone, shifted=False):
+        def half(g, first, backward):
+            xi, yi, zi, vxi, vyi, vzi, qi, ci, ri, mi = (
+                own(row, comp, h, g, 2) for comp in (X, Y, Z, VX, VY, VZ, Q, C, R, MS)
+            )
+            ax, ay, az = (acc[d, row, 1 + h, pl.ds(g * 8, 16), :].reshape(2, 8, LN) for d in range(3))
+            for j in range(first, S):
+                dx = xi - other(r, X, b, h, j)
+                dy = yi - other(r, Y, b, h, j)
+                dz = zi - other(r, Z, b, h, j)
+                n = (
+                    dx * (vxi - other(r, VX, b, h, j))
+                    + dy * (vyi - other(r, VY, b, h, j))
+                    + dz * (vzi - other(r, VZ, b, h, j))
+                )
+                mu = jnp.minimum(n, 0.0) * cache_a[slot * S + j, pl.ds(g, 2)]
+                visc = (mu * (mu - (ci + other(r, C, b, h, j)))) / (ri + other(r, R, b, h, j))
+                f = cache_w[slot * S + j, pl.ds(g, 2)] * (qi + other(r, Q, b, h, j) + visc)
+                fi = f * other(r, MS, b, h, j)
+                ax, ay, az = ax + fi * dx, ay + fi * dy, az + fi * dz
+                if j >= backward:
+                    fj = f * mi
+                    for d, delta in enumerate((dx, dy, dz)):
+                        back_d = fj * delta
+                        back[d, pl.ds(j * 8, 8), :] = back_d[0] + back_d[1]
+            for d, total in enumerate((ax, ay, az)):
+                acc[d, row, 1 + h, pl.ds(g * 8, 16), :] = total.reshape(16, LN)
+            if backward < S:
+                for d in range(3):
+                    give_back(acc.at[d], d, r, b, h, alone, shifted, -1.0)
+
+        if alone:
+            half(0, 0, 16)
+            half(2, 16, S)
+        else:
+
+            def part(i, _):
+                half(i * 2, 0, 0)
+                return 0
+
+            lax.fori_loop(0, 2, part, 0)
+
     def density_stage(stage, k, first=0, last=2):
         per = NACT[k] // 8
         halves = 2 if per == 1 else 1
         base = STAGE_BASE[stage]
 
-        def pairs(c, h):
-            row, r, b = stage_ids(stage, c)
-            xi, yi, zi = (own(row, comp, h, 0, per) for comp in (X, Y, Z))
-            slot = (base + c) * 2 + h
-            total = dens[row, h, pl.ds(0, per * 8), :].reshape(per, 8, LN)
+        def pairs(c, h, edge=False):
+            row, r, b = (2, 4, 0) if edge else stage_ids(stage, c)
+            xi, yi, zi = (own(3 if edge else row, comp, h, 0, per) for comp in (X, Y, Z))
+            slot = EDGE_SLOT if edge else (base + c) * 2 + h
+            total = dens[row, 1 + h, pl.ds(0, per * 8), :].reshape(per, 8, LN)
             for j in range(S):
                 dx = xi - other(r, X, b, h, j)
                 dy = yi - other(r, Y, b, h, j)
@@ -177,7 +312,7 @@
                 total = total + w3 * (s * (5.0 - s))
                 cache_w[slot * S + j, pl.ds(0, per)] = w3
                 cache_a[slot * S + j, pl.ds(0, per)] = 1.0 / (r2 + 0.16)
-            dens[row, h, pl.ds(0, per * 8), :] = total.reshape(per * 8, LN)
+            dens[row, 1 + h, pl.ds(0, per * 8), :] = total.reshape(per * 8, LN)
 
         def combo(i, _):
             if halves == 2:
@@ -187,6 +322,12 @@
                 pairs(i // 2, i % 2)
             return 0
 
+        if k == 0 and stage < 2:
+            paired_stage(stage, density_paired)
+            if stage == 1:
+                pairs(0, 0, edge=True)
+                spread_edges(dens)
+            return
         per_row = STAGE_SIZE[stage] // halves
         lax.fori_loop(first * per_row, last * per_row, combo, 0)
 
@@ -197,13 +338,13 @@
         halves = 2 if per == 1 else 1
         base = STAGE_BASE[stage]
 
-        def pairs(c, h, g):
-            row, r, b = stage_ids(stage, c)
+        def pairs(c, h, g, edge=False):
+            row, r, b = (2, 4, 0) if edge else stage_ids(stage, c)
             xi, yi, zi, vxi, vyi, vzi, qi, ci, ri = (
-                own(row, comp, h, g, per) for comp in (X, Y, Z, VX, VY, VZ, Q, C, R)
+                own(3 if edge else row, comp, h, g, per) for comp in (X, Y, Z, VX, VY, VZ, Q, C, R)
             )
-            slot = (base + c) * 2 + h
-            ax, ay, az = (acc[d, row, h, pl.ds(g * 8, per * 8), :].reshape(per, 8, LN) for d in range(3))
+            slot = EDGE_SLOT if edge else (base + c) * 2 + h
+            ax, ay, az = (acc[d, row, 1 + h, pl.ds(g * 8, per * 8), :].reshape(per, 8, LN) for d in range(3))
             for j in range(S):
                 dx = xi - other(r, X, b, h, j)
                 dy = yi - other(r, Y, b, h, j)
@@ -219,7 +360,7 @@
                 f = cache_w[slot * S + j, pl.ds(g, per)] * (qi + other(r, Q, b, h, j) + visc)
                 ax, ay, az = ax + f * dx, ay + f * dy, az + f * dz
             for d, total in enumerate((ax, ay, az)):
-                acc[d, row, h, pl.ds(g * 8, per * 8), :] = total.reshape(per * 8, LN)
+                acc[d, row, 1 + h, pl.ds(g * 8, per * 8), :] = total.reshape(per * 8, LN)
 
         def combo(i, _):
             if halves == 2:
@@ -230,6 +371,18 @@
                 pairs(ch // 2, ch % 2, g)
             return 0
 
+        if k == 0 and stage < 2:
+            paired_stage(stage, force_paired)
+            if stage == 1:
+
+                def edge(i, _):
+                    pairs(0, 0, i * 2, edge=True)
+                    return 0
+
+                lax.fori_loop(0, 2, edge, 0)
+                for d in range(3):
+                    spread_edges(acc.at[d])
+            return
         per_row = STAGE_SIZE[stage] * sets // halves
         lax.fori_loop(first * per_row, last * per_row, combo, 0)
 
@@ -379,6 +532,8 @@
         copies[5].wait_recv()
         for r in (1, 2):
             sides(loads[r], comps, r, n, rnd, 1, r - 1)
+        if k == 0:
+            edges(comps)
         stage_fn(1, k, 0, 2 if row_done is None else 1)
         for f in (0, 1, 2, 3, 6, 7):
             copies[f].wait_recv()
@@ -443,7 +598,7 @@
                 for d in range(3):
                     v = st[3 + d, row, h, rows, :]
                     x = st[d, row, h, rows, :]
-                    v_new = v + 4.0 * acc[d, row, h, rows, :]
+                    v_new = v + 4.0 * acc[d, row, 1 + h, rows, :]
                     st[3 + d, row, h, rows, :] = jnp.where(active, v_new, v)
                     st[d, row, h, rows, :] = jnp.where(active, x + 0.0125 * v_new, x)
 
@@ -468,7 +623,7 @@
                 for g in range(n // 8):
                     rows = pl.ds(g * 8, 8)
                     slot = lax.broadcasted_iota(jnp.int32, (8, LN), 0) + g * 8
-                    rho4 = jnp.where(slot < count, dens[row, h, rows, :], pr[2, row, h, rows, :])
+                    rho4 = jnp.where(slot < count, dens[row, 1 + h, rows, :], pr[2, row, h, rows, :])
                     root = jnp.exp(jnp.log(rho4 * 0.25) * (1.0 / 3.0))
                     pr[0, row, h, rows, :] = sq[0, row, h, rows, :] / root
                     pr[1, row, h, rows, :] = sq[1, row, h, rows, :] * root
@@ -565,11 +720,11 @@
         out_specs=[pl.BlockSpec(memory_space=pl.ANY), vmem],
         scratch_shapes=[
             pltpu.VMEM((subs, LN // 2, 2, 8, LN), f32),
-            pltpu.VMEM((4 * NF * 6, S, LN), f32),
+            pltpu.VMEM((5 * NF * 6, S, LN), f32),
             pltpu.VMEM((7, 2, 2, S, LN), f32),
             pltpu.VMEM((3, 2, 2, S, LN), f32),
-            pltpu.VMEM((2, 2, S, LN), f32),
-            pltpu.VMEM((3, 2, 2, S, LN), f32),
+            pltpu.VMEM((3, 4, S, LN), f32),
+            pltpu.VMEM((3, 3, 4, S, LN), f32),
             pltpu.VMEM((2, 2, 2, S, LN), f32),
             pltpu.VMEM((6, 2, S, LN), f32),
             pltpu.VMEM((3, 2, 7, 2, S, LN), f32),
@@ -578,6 +733,7 @@
             pltpu.VMEM((18 * 2 * S, 4, 8, LN), f32),
             pltpu.VMEM((18 * 2 * S, 4, 8, LN), f32),
             pltpu.VMEM((4, 256, LN), f32),
+            pltpu.VMEM((3, 256, LN), f32),
             pltpu.VMEM((LN, LN), jnp.int32),
             pltpu.VMEM((subs, 2 * subs, LN), f32),
             pltpu.SemaphoreType.DMA((2, 8)),

time: 101 us -> 96.2 us (0.952)
  Pallas kernels: 101 us -> 96 us
    pallas_call x1, Pallas kernels: 95.6 us -> 90.5 us  [shards(): pl.pallas_call(functools.partial(substeps_kernel, tiles, subs), out_shape...]
where the time goes in v6:
time: 96.2 us; the launch traced here: 96 us
  Pallas kernels  96 us (100%)
    pallas_call x1, Pallas kernels, shards(): pl.pallas_call(functools.partial(substeps_kernel, tiles, subs), out_shape...  90.5 us
    pallas_call x1, Pallas kernels, shards(): pl.pallas_call(lay_kernel, grid=(STEPS,), out_shape=jax.ShapeDtypeStruct(...  5.54 us

profile of v6, /device:TPU:0, one launch (start us, length us, event | category | flops | bytes accessed | tf_op | source)
XLA Modules:
  0.0 96.0 jit_solution(16593015304201689562)
XLA Ops:
  0.0 90.5 %substeps.1 = (f32[4,64,2,8,128]{4,3,2,1,0:T(8,128)}, s32[16,128]{1,0:T(8,128)}) custom-call(f32[3,128,128]{2,1,0:T(8,128)} %bitcast.33, f32[3,128,128]{2,1,0:T(8,128)} %bitcast.34, f32[128,128]{1,0:T(8,128)} %bitcast.35, f32[128,128]{1,0:T(8,128)} %bitcast.36, s32[3,4,128]{2,1,0:T(4,128)} %bitcast.38, s32[128,128]{1,0:T(8,128)} %bitcast.37), custom_call_target="tpu_custom_call" | custom-call | tf_op jit(solution)/shard_map/substeps/pallas_call | solution.py:713
  90.5 5.5 %lay.1 = f32[192,8,128]{2,1,0:T(8,128)} custom-call(s32[16,128]{1,0:T(8,128)} %get-tuple-element.7.runs, f32[4,64,2,8,128]{4,3,2,1,0:T(8,128)} %get-tuple-element.8.gathered), custom_call_target="tpu_custom_call" | custom-call | tf_op jit(solution)/shard_map/lay/pallas_call | solution.py:750

commit v7 on v6

--- a/solution.py
+++ b/solution.py
@@ -467,14 +467,26 @@
         half = rows // 2
         part = pl.ds(first + half * second_half, half)
         which = slice(None) if len(own_rows) == 2 else own_rows[0]
+        landing = done if p >= 2 and flow not in (0, 2) else gathered
         return pltpu.make_async_remote_copy(
             src_ref=gathered.at[owner, part, which],
-            dst_ref=gathered.at[owner, part, which],
+            dst_ref=landing.at[owner, part, which],
             send_sem=piece_send.at[p, flow],
             recv_sem=piece_recv.at[p, flow],
             device_id=(t, dst),
             device_id_type=MESH,
         )
+
+    leaving = []
+
+    def write_out(p, at, owner, first, rows):
+        own_rows = PIECES[p][2]
+        which = slice(None) if len(own_rows) == 2 else own_rows[0]
+        copy = pltpu.make_async_copy(
+            gathered.at[owner, pl.ds(first, rows), which], done.at[owner, pl.ds(first, rows), which], done_sem.at[p, at]
+        )
+        copy.start()
+        leaving.append(copy)
 
     def start_piece(p, before_rest=None):
         first, rows, own_rows = PIECES[p]
@@ -493,6 +505,8 @@
             before_rest()
         copies[1].start()
         copies[3].start()
+        if p >= 2:
+            write_out(p, 0, u, first, rows)
 
     def forward_piece(p):
         arriving[p][0].wait_recv()
@@ -501,21 +515,18 @@
         for copy in copies:
             copy.start()
         arriving[p] += copies
-
-    leaving = []
+        if p >= 2:
+            first, rows, _ = PIECES[p]
+            write_out(p, 1, left, first, rows // 2)
+            write_out(p, 2, right, first + rows // 2, rows // 2)
 
     def finish_piece(p):
         for f in (1, 3, 4, 5):
             arriving[p][f].wait_recv()
         for copy in arriving[p]:
             copy.wait_send()
-        first, rows, own_rows = PIECES[p]
-        which = slice(None) if len(own_rows) == 2 else own_rows[0]
-        copy = pltpu.make_async_copy(
-            gathered.at[:, pl.ds(first, rows), which], done.at[:, pl.ds(first, rows), which], done_sem.at[p]
-        )
-        copy.start()
-        leaving.append(copy)
+        if p < 2:
+            write_out(p, 0, slice(None), PIECES[p][0], PIECES[p][1])
 
     def exchange_and_sum(rnd, src, inbox, comps, n, stage_fn, k, meanwhile, row_done=None):
         copies = start_round(rnd, src, len(comps), n, inbox)
@@ -571,10 +582,10 @@
         base = jnp.dot(padded, earlier, preferred_element_type=jnp.float32)[0:subs]
         base = base.astype(jnp.int32)
         skip = base & (LN - 1)
-        runs[0:subs, :] = (skip - starts.astype(jnp.int32)) & (LN - 1)
-        runs[subs : 2 * subs, :] = skip
-        runs[2 * subs : 3 * subs, :] = skip + counts.astype(jnp.int32)
-        runs[3 * subs : 4 * subs, :] = base >> 7
+        turn = (skip - starts.astype(jnp.int32)) & (LN - 1)
+        end = skip + counts.astype(jnp.int32)
+        runs[0:subs, :] = turn + skip * 128 + end * 16384 + (base >> 7) * 4194304
+        runs[subs : 2 * subs, :] = jnp.zeros((subs, LN), jnp.int32)
 
     def during(rnd):
         if rnd == 0:
@@ -671,11 +682,13 @@
                 at = (step * (S // STEPS) + slot) * 4 + h * 2 + row
                 later = []
                 for src in range(subs):
-                    end = jnp.full((8, LN), runs[2 * subs + src, at])
-                    turned = pltpu.roll(gathered[src, slot * 2 + h, row], runs[src, at], 1)
+                    word = runs[src, at]
+                    words = jnp.full((8, LN), word)
+                    end = (words >> 14) & 255
+                    turned = pltpu.roll(gathered[src, slot * 2 + h, row], word & (LN - 1), 1)
                     kept = jnp.where(lane < end, turned, 0.0)
-                    merged = jnp.where(lane < runs[subs + src, at], currents[src], kept)
-                    tiles[src, runs[3 * subs + src, at]] = merged
+                    merged = jnp.where(lane < ((words >> 7) & (LN - 1)), currents[src], kept)
+                    tiles[src, word >> 22] = merged
                     wrapped = jnp.where(beyond < end, turned, 0.0)
                     later.append(jnp.where(end >= LN, wrapped, merged))
                 currents = later
@@ -688,8 +701,8 @@
     @pl.when(step == STEPS - 1)
     def _():
         for src in range(subs):
-            last = runs[2 * subs + src, LN - 1]
-            tiles[src, runs[3 * subs + src, LN - 1] + jnp.where(last >= LN, 1, 0)] = currents[src]
+            word = runs[src, LN - 1]
+            tiles[src, (word >> 22) + jnp.where((word >> 14) & 255 >= LN, 1, 0)] = currents[src]
         for src in range(subs):
             out[pl.ds(src * TILES, TILES)] = tiles[src, pl.ds(0, TILES)]
 
@@ -714,7 +727,7 @@
         functools.partial(substeps_kernel, tiles, subs),
         out_shape=[
             jax.ShapeDtypeStruct((subs, LN // 2, 2, 8, LN), f32),
-            jax.ShapeDtypeStruct((4 * subs, LN), jnp.int32),
+            jax.ShapeDtypeStruct((2 * subs, LN), jnp.int32),
         ],
         in_specs=[vmem] * 6,
         out_specs=[pl.BlockSpec(memory_space=pl.ANY), vmem],
@@ -742,7 +755,7 @@
             pltpu.SemaphoreType.DMA((4,)),
             pltpu.SemaphoreType.DMA((4, 6)),
             pltpu.SemaphoreType.DMA((4, 6)),
-            pltpu.SemaphoreType.DMA((4,)),
+            pltpu.SemaphoreType.DMA((4, 3)),
         ],
         compiler_params=pltpu.CompilerParams(collective_id=0, has_side_effects=True, vmem_limit_bytes=62 * 1024 * 1024),
         name="substeps",

time: 96.2 us -> 95.6 us (level)
  no operation moved by 1% of the time
where the time goes in v7:
time: 95.6 us; the launch traced here: 95.4 us
  Pallas kernels  95.4 us (100%)
    pallas_call x1, Pallas kernels, shards(): pl.pallas_call(functools.partial(substeps_kernel, tiles, subs), out_shape...  90 us
    pallas_call x1, Pallas kernels, shards(): pl.pallas_call(lay_kernel, grid=(STEPS,), out_shape=jax.ShapeDtypeStruct(...  5.38 us

profile of v7, /device:TPU:0, one launch (start us, length us, event | category | flops | bytes accessed | tf_op | source)
XLA Modules:
  0.0 95.4 jit_solution(9229432479930967286)
XLA Ops:
  0.0 90.0 %substeps.1 = (f32[4,64,2,8,128]{4,3,2,1,0:T(8,128)}, s32[8,128]{1,0:T(8,128)}) custom-call(f32[3,128,128]{2,1,0:T(8,128)} %bitcast.33, f32[3,128,128]{2,1,0:T(8,128)} %bitcast.34, f32[128,128]{1,0:T(8,128)} %bitcast.35, f32[128,128]{1,0:T(8,128)} %bitcast.36, s32[3,4,128]{2,1,0:T(4,128)} %bitcast.38, s32[128,128]{1,0:T(8,128)} %bitcast.37), custom_call_target="tpu_custom_call" | custom-call | tf_op jit(solution)/shard_map/substeps/pallas_call | solution.py:726
  90.0 5.4 %lay.1 = f32[192,8,128]{2,1,0:T(8,128)} custom-call(s32[8,128]{1,0:T(8,128)} %get-tuple-element.7.runs, f32[4,64,2,8,128]{4,3,2,1,0:T(8,128)} %get-tuple-element.8.gathered), custom_call_target="tpu_custom_call" | custom-call | tf_op jit(solution)/shard_map/lay/pallas_call | solution.py:763

commit v8 on v7

--- a/solution.py
+++ b/solution.py
@@ -41,8 +41,9 @@
 
 
 def substeps_kernel(
-    tiles, subs, off, vel, mass, ent, cnt, tgt, done, runs, gathered, fld, st, pr, dens, acc, sq, ysend, xin, pin, yin,
-    cache_w, cache_a, raw, back, pos, tab, send_sem, recv_sem, tab_send, tab_recv, piece_send, piece_recv, done_sem
+    tiles, subs, off_in, vel_in, mass_in, ent_in, cnt_in, tgt_in, done, runs_out, gathered, off, vel, mass, ent, cnt,
+    tgt, runs, fld, st, pr, dens, acc, sq, ysend, xin, pin, yin,
+    cache_w, cache_a, raw, back, pos, tab, send_sem, recv_sem, tab_send, tab_recv, piece_send, piece_recv, done_sem, in_sem, runs_sem
 ):
     t, u = lax.axis_index("tile"), lax.axis_index("sub")
     up, down = lax.rem(t + 1, tiles), lax.rem(t + tiles - 1, tiles)
@@ -54,6 +55,17 @@
     near = ((down, u), (up, u), (down, left), (t, left), (up, left), (down, right), (t, right), (up, right))
     for dev in near + ((t, across),):
         pl.semaphore_signal(barrier, inc=1, device_id=dev, device_id_type=MESH)
+
+    inputs = [
+        pltpu.make_async_copy(src, dst, in_sem.at[i])
+        for i, (src, dst) in enumerate(
+            ((cnt_in, cnt), (off_in, off), (vel_in, vel), (mass_in, mass), (ent_in, ent), (tgt_in, tgt))
+        )
+    ]
+    for copy in inputs:
+        copy.start()
+    for copy in inputs:
+        copy.wait()
 
     for row in range(2):
         for h in range(2):
@@ -586,6 +598,8 @@
         end = skip + counts.astype(jnp.int32)
         runs[0:subs, :] = turn + skip * 128 + end * 16384 + (base >> 7) * 4194304
         runs[subs : 2 * subs, :] = jnp.zeros((subs, LN), jnp.int32)
+        arriving["runs"] = pltpu.make_async_copy(runs, runs_out, runs_sem)
+        arriving["runs"].start()
 
     def during(rnd):
         if rnd == 0:
@@ -657,6 +671,7 @@
         finish_piece(p)
     for copy in leaving:
         copy.wait()
+    arriving["runs"].wait()
 
 
 TILES = 48
@@ -665,21 +680,25 @@
 STEPS = 4
 
 
-def lay_kernel(runs, gathered, out, tiles, edge):
+def lay_kernel(runs, gathered_in, out, gathered, tiles, in_sem, out_sem):
     subs = gathered.shape[0]
     lane = lane_iota()
     beyond = lane + LN
-    step = pl.program_id(0)
-
-    @pl.when(step == 0)
-    def _():
-        tiles[...] = jnp.zeros_like(tiles)
-        edge[...] = jnp.zeros_like(edge)
+    block = LN // 2 // STEPS
+    inputs = [
+        pltpu.make_async_copy(
+            gathered_in.at[:, pl.ds(i * block, block)], gathered.at[:, pl.ds(i * block, block)], in_sem.at[i]
+        )
+        for i in range(STEPS)
+    ]
+    for copy in inputs:
+        copy.start()
+    tiles[...] = jnp.zeros_like(tiles)
 
     def lay(slot, currents):
         for row in range(2):
             for h in range(2):
-                at = (step * (S // STEPS) + slot) * 4 + h * 2 + row
+                at = slot * 4 + h * 2 + row
                 later = []
                 for src in range(subs):
                     word = runs[src, at]
@@ -694,17 +713,22 @@
                 currents = later
         return tuple(currents)
 
-    currents = lax.fori_loop(0, S // STEPS, lay, tuple(edge[src] for src in range(subs)))
+    currents = (jnp.zeros((8, LN), jnp.float32),) * subs
+    for i in range(STEPS):
+        inputs[i].wait()
+        currents = lax.fori_loop(i * (S // STEPS), (i + 1) * (S // STEPS), lay, currents)
+    outputs = []
     for src in range(subs):
-        edge[src] = currents[src]
-
-    @pl.when(step == STEPS - 1)
-    def _():
-        for src in range(subs):
-            word = runs[src, LN - 1]
-            tiles[src, (word >> 22) + jnp.where((word >> 14) & 255 >= LN, 1, 0)] = currents[src]
-        for src in range(subs):
-            out[pl.ds(src * TILES, TILES)] = tiles[src, pl.ds(0, TILES)]
+        word = runs[src, LN - 1]
+        tiles[src, (word >> 22) + jnp.where((word >> 14) & 255 >= LN, 1, 0)] = currents[src]
+    for src in range(subs):
+        copy = pltpu.make_async_copy(
+            tiles.at[src, pl.ds(0, TILES)], out.at[pl.ds(src * TILES, TILES)], out_sem.at[src]
+        )
+        copy.start()
+        outputs.append(copy)
+    for copy in outputs:
+        copy.wait()
 
 
 def rows_of(a):
@@ -721,7 +745,7 @@
     ent = rows_of(entropy).reshape(LN, LN)
     cnt = rows_of(active_counts).reshape(3, 4, LN)
     tgt = rows_of(targets).reshape(LN, LN)
-    vmem = pl.BlockSpec(memory_space=pltpu.VMEM)
+    anywhere = pl.BlockSpec(memory_space=pl.ANY)
     f32 = jnp.float32
     gathered, runs = pl.pallas_call(
         functools.partial(substeps_kernel, tiles, subs),
@@ -729,10 +753,17 @@
             jax.ShapeDtypeStruct((subs, LN // 2, 2, 8, LN), f32),
             jax.ShapeDtypeStruct((2 * subs, LN), jnp.int32),
         ],
-        in_specs=[vmem] * 6,
-        out_specs=[pl.BlockSpec(memory_space=pl.ANY), vmem],
+        in_specs=[anywhere] * 6,
+        out_specs=[anywhere] * 2,
         scratch_shapes=[
             pltpu.VMEM((subs, LN // 2, 2, 8, LN), f32),
+            pltpu.VMEM((3, LN, LN), f32),
+            pltpu.VMEM((3, LN, LN), f32),
+            pltpu.VMEM((LN, LN), f32),
+            pltpu.VMEM((LN, LN), f32),
+            pltpu.VMEM((3, 4, LN), jnp.int32),
+            pltpu.VMEM((LN, LN), jnp.int32),
+            pltpu.VMEM((2 * subs, LN), jnp.int32),
             pltpu.VMEM((5 * NF * 6, S, LN), f32),
             pltpu.VMEM((7, 2, 2, S, LN), f32),
             pltpu.VMEM((3, 2, 2, S, LN), f32),
@@ -756,20 +787,23 @@
             pltpu.SemaphoreType.DMA((4, 6)),
             pltpu.SemaphoreType.DMA((4, 6)),
             pltpu.SemaphoreType.DMA((4, 3)),
+            pltpu.SemaphoreType.DMA((6,)),
+            pltpu.SemaphoreType.DMA,
         ],
         compiler_params=pltpu.CompilerParams(collective_id=0, has_side_effects=True, vmem_limit_bytes=62 * 1024 * 1024),
         name="substeps",
     )(off, vel, mas, ent, cnt, tgt)
     arrived = pl.pallas_call(
         lay_kernel,
-        grid=(STEPS,),
         out_shape=jax.ShapeDtypeStruct((subs * TILES, 8, LN), f32),
-        in_specs=[
-            pl.BlockSpec(memory_space=pltpu.SMEM),
-            pl.BlockSpec((subs, LN // 2 // STEPS, 2, 8, LN), lambda i: (0, i, 0, 0, 0)),
+        in_specs=[pl.BlockSpec(memory_space=pltpu.SMEM), anywhere],
+        out_specs=anywhere,
+        scratch_shapes=[
+            pltpu.VMEM((subs, LN // 2, 2, 8, LN), f32),
+            pltpu.VMEM((subs, TILES + 2, 8, LN), f32),
+            pltpu.SemaphoreType.DMA((STEPS,)),
+            pltpu.SemaphoreType.DMA((subs,)),
         ],
-        out_specs=pl.BlockSpec((subs * TILES, 8, LN), lambda i: (0, 0, 0)),
-        scratch_shapes=[pltpu.VMEM((subs, TILES + 2, 8, LN), f32), pltpu.VMEM((subs, 8, LN), f32)],
         name="lay",
     )(runs, gathered)
     return jnp.transpose(arrived, (1, 0, 2)).reshape(8, subs * TILES * LN)

time: 95.6 us -> 94.3 us (0.986)
  Pallas kernels: 95.4 us -> 94.1 us
    pallas_call x1, Pallas kernels: 90 us -> 88.5 us  [shards(): pl.pallas_call(functools.partial(substeps_kernel, tiles, subs), out_shape...]
where the time goes in v8:
time: 94.3 us; the launch traced here: 94.1 us
  Pallas kernels  94.1 us (100%)
    pallas_call x1, Pallas kernels, shards(): pl.pallas_call(functools.partial(substeps_kernel, tiles, subs), out_shape...  88.5 us
    pallas_call x1, Pallas kernels, shards(): pl.pallas_call(lay_kernel, out_shape=jax.ShapeDtypeStruct((subs * TILES,...  5.59 us

profile of v8, /device:TPU:0, one launch (start us, length us, event | category | flops | bytes accessed | tf_op | source)
XLA Modules:
  0.0 94.1 jit_solution(691716747017252564)
XLA Ops:
  0.0 88.5 %substeps.1 = (f32[4,64,2,8,128]{4,3,2,1,0:T(8,128)}, s32[8,128]{1,0:T(8,128)}) custom-call(f32[3,128,128]{2,1,0:T(8,128)} %bitcast.33, f32[3,128,128]{2,1,0:T(8,128)} %bitcast.34, f32[128,128]{1,0:T(8,128)} %bitcast.35, f32[128,128]{1,0:T(8,128)} %bitcast.36, s32[3,4,128]{2,1,0:T(4,128)} %bitcast.38, s32[128,128]{1,0:T(8,128)} %bitcast.37), custom_call_target="tpu_custom_call" | custom-call | tf_op jit(solution)/shard_map/substeps/pallas_call | solution.py:750
  88.5 5.6 %lay.1 = f32[192,8,128]{2,1,0:T(8,128)} custom-call(s32[8,128]{1,0:T(8,128)} %get-tuple-element.7.runs, f32[4,64,2,8,128]{4,3,2,1,0:T(8,128)} %get-tuple-element.8.gathered_in), custom_call_target="tpu_custom_call" | custom-call | tf_op jit(solution)/shard_map/lay/pallas_call | solution.py:796

commit v9 on v8

--- a/solution.py
+++ b/solution.py
@@ -680,7 +680,7 @@
 STEPS = 4
 
 
-def lay_kernel(runs, gathered_in, out, gathered, tiles, in_sem, out_sem):
+def lay_kernel(runs_in, gathered_in, out, runs, gathered, tiles, runs_sem, in_sem, out_sem):
     subs = gathered.shape[0]
     lane = lane_iota()
     beyond = lane + LN
@@ -691,9 +691,12 @@
         )
         for i in range(STEPS)
     ]
-    for copy in inputs:
-        copy.start()
+    table = pltpu.make_async_copy(runs_in, runs, runs_sem)
+    table.start()
+    inputs[0].start()
+    inputs[1].start()
     tiles[...] = jnp.zeros_like(tiles)
+    table.wait()
 
     def lay(slot, currents):
         for row in range(2):
@@ -716,6 +719,8 @@
     currents = (jnp.zeros((8, LN), jnp.float32),) * subs
     for i in range(STEPS):
         inputs[i].wait()
+        if i + 2 < STEPS:
+            inputs[i + 2].start()
         currents = lax.fori_loop(i * (S // STEPS), (i + 1) * (S // STEPS), lay, currents)
     outputs = []
     for src in range(subs):
@@ -796,11 +801,13 @@
     arrived = pl.pallas_call(
         lay_kernel,
         out_shape=jax.ShapeDtypeStruct((subs * TILES, 8, LN), f32),
-        in_specs=[pl.BlockSpec(memory_space=pltpu.SMEM), anywhere],
+        in_specs=[anywhere] * 2,
         out_specs=anywhere,
         scratch_shapes=[
+            pltpu.SMEM((2 * subs, LN), jnp.int32),
             pltpu.VMEM((subs, LN // 2, 2, 8, LN), f32),
             pltpu.VMEM((subs, TILES + 2, 8, LN), f32),
+            pltpu.SemaphoreType.DMA,
             pltpu.SemaphoreType.DMA((STEPS,)),
             pltpu.SemaphoreType.DMA((subs,)),
         ],

time: 94.3 us -> 93.6 us (level)
  no operation moved by 1% of the time
where the time goes in v9:
time: 93.6 us; the launch traced here: 93.4 us
  Pallas kernels  93.4 us (100%)
    pallas_call x1, Pallas kernels, shards(): pl.pallas_call(functools.partial(substeps_kernel, tiles, subs), out_shape...  88.5 us
    pallas_call x1, Pallas kernels, shards(): pl.pallas_call(lay_kernel, out_shape=jax.ShapeDtypeStruct((subs * TILES,...  4.88 us

profile of v9, /device:TPU:0, one launch (start us, length us, event | category | flops | bytes accessed | tf_op | source)
XLA Modules:
  0.0 93.4 jit_solution(1526567498881584787)
XLA Ops:
  0.0 88.5 %substeps.1 = (f32[4,64,2,8,128]{4,3,2,1,0:T(8,128)}, s32[8,128]{1,0:T(8,128)}) custom-call(f32[3,128,128]{2,1,0:T(8,128)} %bitcast.33, f32[3,128,128]{2,1,0:T(8,128)} %bitcast.34, f32[128,128]{1,0:T(8,128)} %bitcast.35, f32[128,128]{1,0:T(8,128)} %bitcast.36, s32[3,4,128]{2,1,0:T(4,128)} %bitcast.38, s32[128,128]{1,0:T(8,128)} %bitcast.37), custom_call_target="tpu_custom_call" | custom-call | tf_op jit(solution)/shard_map/substeps/pallas_call | solution.py:755
  88.5 4.9 %lay.1 = f32[192,8,128]{2,1,0:T(8,128)} custom-call(s32[8,128]{1,0:T(8,128)} %get-tuple-element.7.runs_in, f32[4,64,2,8,128]{4,3,2,1,0:T(8,128)} %get-tuple-element.8.gathered_in), custom_call_target="tpu_custom_call" | custom-call | tf_op jit(solution)/shard_map/lay/pallas_call | solution.py:801

commit v10 on v9

--- a/solution.py
+++ b/solution.py
@@ -604,14 +604,14 @@
     def during(rnd):
         if rnd == 0:
             arriving["tab"] = plan()
-        elif rnd == 1:
-            lay_plan()
         elif rnd in (2, 4):
             if rnd == 4:
                 finish_piece(0)
             start_piece(rnd // 2 - 1)
         elif rnd in (3, 5):
             forward_piece(rnd // 2 - 1)
+            if rnd == 5:
+                lay_plan()
 
     def move(k, row):
         for h in range(2):
@@ -721,7 +721,7 @@
         inputs[i].wait()
         if i + 2 < STEPS:
             inputs[i + 2].start()
-        currents = lax.fori_loop(i * (S // STEPS), (i + 1) * (S // STEPS), lay, currents)
+        currents = lax.fori_loop(i * (S // STEPS), (i + 1) * (S // STEPS), lay, currents, unroll=2)
     outputs = []
     for src in range(subs):
         word = runs[src, LN - 1]

time: 93.6 us -> 92.6 us (0.989)
  Pallas kernels: 93.4 us -> 92.4 us
where the time goes in v10:
time: 92.6 us; the launch traced here: 92.4 us
  Pallas kernels  92.4 us (100%)
    pallas_call x1, Pallas kernels, shards(): pl.pallas_call(functools.partial(substeps_kernel, tiles, subs), out_shape...  88.4 us
    pallas_call x1, Pallas kernels, shards(): pl.pallas_call(lay_kernel, out_shape=jax.ShapeDtypeStruct((subs * TILES,...  4.01 us

profile of v10, /device:TPU:0, one launch (start us, length us, event | category | flops | bytes accessed | tf_op | source)
XLA Modules:
  0.0 92.4 jit_solution(12017344080427831272)
XLA Ops:
  0.0 88.4 %substeps.1 = (f32[4,64,2,8,128]{4,3,2,1,0:T(8,128)}, s32[8,128]{1,0:T(8,128)}) custom-call(f32[3,128,128]{2,1,0:T(8,128)} %bitcast.33, f32[3,128,128]{2,1,0:T(8,128)} %bitcast.34, f32[128,128]{1,0:T(8,128)} %bitcast.35, f32[128,128]{1,0:T(8,128)} %bitcast.36, s32[3,4,128]{2,1,0:T(4,128)} %bitcast.38, s32[128,128]{1,0:T(8,128)} %bitcast.37), custom_call_target="tpu_custom_call" | custom-call | tf_op jit(solution)/shard_map/substeps/pallas_call | solution.py:755
  88.4 4.0 %lay.1 = f32[192,8,128]{2,1,0:T(8,128)} custom-call(s32[8,128]{1,0:T(8,128)} %get-tuple-element.7.runs_in, f32[4,64,2,8,128]{4,3,2,1,0:T(8,128)} %get-tuple-element.8.gathered_in), custom_call_target="tpu_custom_call" | custom-call | tf_op jit(solution)/shard_map/lay/pallas_call | solution.py:801
